TPU v7x, 128 devices: a whole 4x4x4 slice. The times are simulated.
128 devices in a mesh: day: 16 (over x, y), pair: 8 (over z, core).
Axes of the slice: x: 4, y: 4, z: 4, core: 2. Of those that a mesh axis runs over, the one named last changes fastest.
Arguments:
- correlations: bfloat16 [64, 4096, 2001], P('day', 'pair'), may hold values from -8 to 8
- mask: int32 [64, 4096], P('day', 'pair'), may hold values from 0 to 1, as said below
- counts: int32 [4096], P(('pair', 'day')), may hold values from 1 to 64, as said below
Outputs:
- phase_weighted: float32 [4096, 2001], P(('pair', 'day'))
- linear: float32 [4096, 2001], P(('pair', 'day'))
Inputs may be any that keep to these rules, and one draw needn't show every extreme that they name: `mask`: every pair has a usable correlation on at least one day. counts[p] equals the number of days d with mask[d, p] = 1.
All inputs are finite; a program needn't handle non-finite values.
Results may differ from a plain program's by a relative error of at most 0.00044.
Values may be sent and summed in bfloat16 or wider, within the bound.
No kernel may reach another device: no remote copies, remote signals or barrier semaphores. Data moves between devices by JAX's collectives and lax.ppermute only.
A program may use at most 128 MiB of HBM per device.

v0:
```python
import functools

import jax
import jax.numpy as jnp
from jax import lax
from jax.experimental import pallas as pl
from jax.experimental.pallas import tpu as pltpu
from jax.sharding import PartitionSpec as P


LAGS = 2001
WIDTH = 2048
WORDS = WIDTH // 2
OWNED = 32
DAYS = 4
SIDE = 4
QUANTITIES = 3
TOP = 32766.0
KERNEL_SUM = 6.0
MB = 1 << 20


def params(**settings):
    return pltpu.CompilerParams(**{"vmem_limit_bytes": 32 * MB, **settings})


def encode(value, scale):
    root = value * lax.rsqrt(jnp.abs(value) + 1e-36)
    return (root * scale + 32768.5).astype(jnp.int32)


def pack(low, high):
    return low | (high << 16)


def unpack(word):
    low = (word & 0xFFFF).astype(jnp.float32) - 32768.0
    high = (lax.shift_right_logical(word, 16)).astype(jnp.float32) - 32768.0
    return low * jnp.abs(low), high * jnp.abs(high)


def unit(exponent):
    return jnp.exp2(exponent.astype(jnp.float32)) * (1.0 / (TOP * TOP))


def first_shifts():
    row = lax.broadcasted_iota(jnp.int32, (8, 2 * WIDTH), 0)
    col = lax.broadcasted_iota(jnp.int32, (8, 2 * WIDTH), 1)
    offset = (col - row - WIDTH + 2 * LAGS) % LAGS
    offset = jnp.where(offset > LAGS // 2, offset - LAGS, offset)
    angle = jnp.pi * offset.astype(jnp.float32) / LAGS
    parity = 1.0 - 2.0 * (offset % 2).astype(jnp.float32)
    sine = jnp.where(offset == 0, 1.0, jnp.sin(angle))
    values = jnp.where(offset == 0, 0.0, (jnp.cos(angle) - parity) / (LAGS * sine))
    return values.astype(jnp.bfloat16).astype(jnp.float32)


def fill_table(shifts_ref, table_ref, rolled_ref):
    for q in range(16):
        first = pltpu.roll(shifts_ref[...], 16 * q, 1)
        second = pltpu.roll(shifts_ref[...], 16 * q + 8, 1)
        rolled_ref[16 * q : 16 * q + 16, :] = jnp.concatenate([first, second], 0).astype(jnp.bfloat16)
    for q in range(8):
        for n in range(8):
            for h in range(2):
                start = 128 * (n + 8 * h) - 256 * q + WIDTH
                table_ref[n, 256 * q : 256 * q + 256, 128 * h : 128 * h + 128] = rolled_ref[:, start : start + 128]


TILES = WIDTH // 128
GROUPS = 16


def position(owner, place):
    x, y, core = place >> 3, (place >> 1) & 3, place & 1
    along_x, along_y = (owner // SIDE - x) & 3, (owner % SIDE - y) & 3
    return jnp.where(core == 0, along_x * SIDE + along_y, along_y * SIDE + along_x)


def energy_kernel(place_ref, input_ref, given_ref, shifts_ref, *refs):
    held_ref, mask_ref, stats_ref, peak_ref, sems = refs
    last = (LAGS - 128 * (TILES - 1)) * GROUPS

    def fetch(j, size):
        return pltpu.make_async_copy(
            input_ref.at[pl.ds(j * 128 * GROUPS, size), :], held_ref.at[j, pl.ds(0, size), :], sems.at[j]
        )

    mask_copy = pltpu.make_async_copy(given_ref, mask_ref, sems.at[TILES])
    mask_copy.start()
    for j in range(TILES):
        fetch(j, 128 * GROUPS if j < TILES - 1 else last).start()
    held_ref[TILES - 1, last:, :] = jnp.zeros((128 * GROUPS - last, 128), jnp.bfloat16)

    def tile(j, carry):
        total, most = carry
        for b in range(8):
            values = held_ref[j, 256 * b : 256 * b + 256, :].astype(jnp.float32)
            squares = (values * values).reshape(16, GROUPS, 128)
            total += jnp.sum(squares, axis=0)
            most = jnp.maximum(most, jnp.max(squares, axis=0))
        return total, most

    def step(j, carry):
        fetch(j, 128 * GROUPS).wait()
        return tile(j, carry)

    zero = jnp.zeros((GROUPS, 128), jnp.float32)
    carry = lax.fori_loop(0, TILES - 1, step, (zero, zero))
    fetch(TILES - 1, last).wait()
    total, most = tile(TILES - 1, carry)
    mask_copy.wait()
    used = jnp.concatenate([mask_ref[:, 128 * t : 128 * t + 128] for t in range(4)], 0).astype(jnp.float32)
    total, most = total * used, most * used

    row = lax.broadcasted_iota(jnp.int32, (8, 128), 0)
    day = lax.broadcasted_iota(jnp.int32, (GROUPS, 128), 0) % DAYS
    stats = peaks = jnp.zeros((8, 128), jnp.float32)
    for d in range(DAYS):
        stats = jnp.where(row == d, jnp.sum(jnp.where(day == d, total, 0.0)), stats)
        stats = jnp.where(row == DAYS + d, jnp.sum(jnp.where(day == d, used, 0.0)), stats)
        peaks = jnp.where(row == d, jnp.max(jnp.where(day == d, most, 0.0)), peaks)
    peak_ref[...] = peaks
    stats_ref[...] = stats


def energies(place, correlations, mask, shifts):
    stored = correlations.reshape(DAYS, 4, 128, LAGS).transpose(3, 1, 0, 2).reshape(LAGS * GROUPS, 128)
    vmem, hbm = pl.BlockSpec(memory_space=pltpu.VMEM), pl.BlockSpec(memory_space=pltpu.HBM)
    return pl.pallas_call(
        energy_kernel,
        in_specs=[pl.BlockSpec(memory_space=pltpu.SMEM), hbm, hbm, vmem],
        out_specs=[vmem] * 4,
        out_shape=[
            jax.ShapeDtypeStruct((TILES, 128 * GROUPS, 128), jnp.bfloat16),
            jax.ShapeDtypeStruct(mask.shape, mask.dtype),
            jax.ShapeDtypeStruct((8, 128), jnp.float32),
            jax.ShapeDtypeStruct((8, 128), jnp.float32),
        ],
        scratch_shapes=[pltpu.SemaphoreType.DMA((TILES + 1,))],
        compiler_params=params(vmem_limit_bytes=12 * MB),
        name="energy",
    )(
        place,
        pltpu.with_memory_space_constraint(stored, pltpu.HBM),
        pltpu.with_memory_space_constraint(mask, pltpu.HBM),
        shifts,
    )


def rows_kernel(first_tile, last_tile, place_ref, held_ref, mask_ref, *refs):
    out_ref = refs[-1]
    place = place_ref[0]
    row = lax.broadcasted_iota(jnp.int32, (256, 256), 0)
    col = lax.broadcasted_iota(jnp.int32, (256, 256), 1)
    select = ((row // 16 == col % 16) & (row % 16 == col // 16)).astype(jnp.float32).astype(jnp.bfloat16)
    places = [position(owner, place) for owner in range(SIDE * SIDE)]

    def tile(j, carry):
        parts = []
        for b in range(4):
            first = held_ref[j, 512 * b : 512 * b + 256, :]
            second = held_ref[j, 512 * b + 256 : 512 * b + 512, :]
            parts.append(
                jnp.dot(select, jnp.concatenate([first, second], 1), preferred_element_type=jnp.float32)
            )
        for t in range(4):
            for d in range(DAYS):
                at = 16 * (t * DAYS + d)
                pieces = [p[at : at + 16, 128 * h : 128 * h + 128] for p in parts for h in range(2)]
                used = mask_ref[d : d + 1, 128 * t : 128 * t + 128].astype(jnp.float32)
                turned = (jnp.concatenate(pieces, 0) * used).astype(jnp.bfloat16).T
                for i in range(4):
                    lanes = pl.ds(pl.multiple_of(j * 128, 128), 128)
                    out_ref[places[t * 4 + i], d, :, lanes] = turned[OWNED * i : OWNED * i + OWNED, :]
        return carry

    lax.fori_loop(first_tile, last_tile, tile, 0)


def ordered_rows(place, held, mask, before=None):
    vmem = pl.BlockSpec(memory_space=pltpu.VMEM)
    tiles = (0, TILES // 2) if before is None else (TILES // 2, TILES)
    started = [] if before is None else [before]
    return pl.pallas_call(
        functools.partial(rows_kernel, *tiles),
        in_specs=[pl.BlockSpec(memory_space=pltpu.SMEM)] + [vmem] * (2 + len(started)),
        out_specs=vmem,
        out_shape=jax.ShapeDtypeStruct((SIDE * SIDE, DAYS, OWNED, WIDTH), jnp.bfloat16),
        input_output_aliases={3: 0} if started else {},
        compiler_params=params(vmem_limit_bytes=12 * MB),
        cost_estimate=pl.CostEstimate(flops=4 * 10**9, bytes_accessed=8 * MB, transcendentals=0),
        name="rows",
    )(place, held, mask, *started)


def kernel_table(shifts):
    vmem = pl.BlockSpec(memory_space=pltpu.VMEM)
    return pl.pallas_call(
        fill_table,
        in_specs=[vmem],
        out_specs=vmem,
        out_shape=jax.ShapeDtypeStruct((8, WIDTH, 256), jnp.bfloat16),
        scratch_shapes=[pltpu.VMEM((256, 2 * WIDTH), jnp.bfloat16)],
        compiler_params=params(vmem_limit_bytes=12 * MB),
        cost_estimate=pl.CostEstimate(flops=10**9, bytes_accessed=8 * MB, transcendentals=0),
        name="table",
    )(shifts)


def add_kernel(a_ref, b_ref, out_ref):
    out_ref[...] = a_ref[...] + b_ref[...]


def add(a, b):
    vmem = pl.BlockSpec(memory_space=pltpu.VMEM)
    return pl.pallas_call(
        add_kernel,
        in_specs=[vmem] * 2,
        out_specs=vmem,
        out_shape=jax.ShapeDtypeStruct(a.shape, a.dtype),
        compiler_params=params(vmem_limit_bytes=MB),
        name="add",
    )(a, b)


def terms_kernel(k, first, count, rows_ref, table_ref, stats_ref, others_ref, peak_ref, out_ref, even_ref, odd_ref):
    total = stats_ref[...] + others_ref[...]
    energy, used = total[:DAYS, :], total[DAYS:, :]
    weight = lax.rsqrt(energy / (LAGS * jnp.maximum(used, 1.0)) + 0.1)
    reach = weight * jnp.sqrt(peak_ref[:DAYS, :])
    bounds = [
        jnp.sum(reach, axis=0, keepdims=True),
        jnp.sum(jnp.minimum(1.0, 2.0 * reach), axis=0, keepdims=True),
        jnp.sum(jnp.minimum(1.0, 2.0 * KERNEL_SUM * reach), axis=0, keepdims=True),
    ]
    powers = [jnp.ceil(jnp.log(jnp.maximum(v, 1e-30) * 1.001) * 1.4426951) for v in bounds]
    scale = [TOP * jnp.exp2(-0.5 * p) for p in powers]
    row = lax.broadcasted_iota(jnp.int32, (8, 128), 0)
    exponents = jnp.where(row == 0, powers[0], jnp.where(row == 1, powers[1], powers[2])).astype(jnp.int32)
    for n in range(WORDS // 128):
        out_ref[count * QUANTITIES * OWNED :, 128 * n : 128 * n + 128] = exponents
    weights = [weight[d : d + 1, :] for d in range(DAYS)]
    floor = 0.25 / (weight * weight)
    floors = [floor[d : d + 1, :] for d in range(DAYS)]
    base = first * DAYS * OWNED

    def product(n, to_ref):
        to_ref[...] = jnp.dot(
            rows_ref[k, base : base + count * DAYS * OWNED, :], table_ref[n], preferred_element_type=jnp.float32
        )

    def finish_block(n, hilbert_ref):
        for l in range(count):
            codes = []
            for h in range(2):
                lanes = pl.ds(pl.multiple_of(n * 128 + h * WORDS, 128), 128)
                linear = real = imag = None
                for d in range(DAYS):
                    at = (l * DAYS + d) * OWNED
                    x = rows_ref[k, base + at : base + at + OWNED, lanes].astype(jnp.float32)
                    y = hilbert_ref[at : at + OWNED, 128 * h : 128 * h + 128]
                    inverse = lax.rsqrt(x * x + (y * y + floors[d]))
                    a, b = x * inverse, y * inverse
                    linear = x * weights[d] if d == 0 else linear + x * weights[d]
                    real = a if d == 0 else real + a
                    imag = b if d == 0 else imag + b
                codes.append([encode(v, scale[q]) for q, v in enumerate((linear, real, imag))])
            for q in range(QUANTITIES):
                at = (l * QUANTITIES + q) * OWNED
                out_ref[at : at + OWNED, pl.ds(pl.multiple_of(n * 128, 128), 128)] = pack(codes[0][q], codes[1][q])

    def step(i, carry):
        product(2 * i + 1, odd_ref)
        finish_block(2 * i, even_ref)
        product(2 * i + 2, even_ref)
        finish_block(2 * i + 1, odd_ref)
        return carry

    product(0, even_ref)
    lax.fori_loop(0, 3, step, 0)
    product(7, odd_ref)
    finish_block(6, even_ref)
    finish_block(7, odd_ref)


def terms(k, first, count, rows, table, *stats):
    vmem = pl.BlockSpec(memory_space=pltpu.VMEM)
    return pl.pallas_call(
        functools.partial(terms_kernel, k, first, count),
        in_specs=[vmem] * 5,
        out_specs=vmem,
        out_shape=jax.ShapeDtypeStruct((count * QUANTITIES * OWNED + 8, WORDS), jnp.int32),
        scratch_shapes=[pltpu.VMEM((count * DAYS * OWNED, 256), jnp.float32)] * 2,
        compiler_params=params(vmem_limit_bytes=24 * MB),
        cost_estimate=pl.CostEstimate(
            flops=2 * count * DAYS * OWNED * WIDTH * WIDTH, bytes_accessed=12 * MB, transcendentals=0
        ),
        name="terms",
    )(rows, table, *stats)


def decode(message_ref, at, exponent, cols):
    k = unit(exponent)
    low, high = unpack(message_ref[at : at + OWNED, cols])
    return low * k, high * k


def gather_kernel(cuts, blocks, *refs):
    refs, (out_ref, top_ref) = list(refs[:-2]), refs[-2:]
    messages = [[refs.pop(0) for _ in range(cut)] for cut in cuts]
    heads = [parts[0].shape[0] - 8 for parts in messages]
    top = None
    for parts, head in zip(messages, heads):
        exponents = parts[0][head : head + 8, :128]
        top = exponents if top is None else jnp.maximum(top, exponents)
    top_ref[...] = top
    for l in range(blocks):
        for j in range(WORDS // 128):
            cols = slice(128 * j, 128 * j + 128)
            for q in range(QUANTITIES):
                low = high = None
                for parts, head in zip(messages, heads):
                    each = blocks // len(parts)
                    at = (l % each * QUANTITIES + q) * OWNED
                    exponent = parts[0][head + q : head + q + 1, :128]
                    a, b = decode(parts[l // each], at, exponent, cols)
                    low = a if low is None else low + a
                    high = b if high is None else high + b
                at = (l * QUANTITIES + q) * OWNED
                out_ref[at : at + OWNED, cols] = low
                out_ref[at : at + OWNED, 128 * j + WORDS : 128 * j + WORDS + 128] = high


def gather(messages, blocks):
    vmem = pl.BlockSpec(memory_space=pltpu.VMEM)
    parts = [part for message in messages for part in message]
    return pl.pallas_call(
        functools.partial(gather_kernel, [len(message) for message in messages], blocks),
        in_specs=[vmem] * len(parts),
        out_specs=[vmem] * 2,
        out_shape=[
            jax.ShapeDtypeStruct((blocks * QUANTITIES * OWNED, WIDTH), jnp.float32),
            jax.ShapeDtypeStruct((8, 128), jnp.int32),
        ],
        compiler_params=params(vmem_limit_bytes=16 * MB),
        cost_estimate=pl.CostEstimate(flops=blocks * MB, bytes_accessed=2 * MB, transcendentals=0),
        name="gather",
    )(*parts)


def combine_kernel(l, sums_ref, top_ref, *refs):
    messages, out_ref = refs[:-1], refs[-1]
    heads = [message.shape[0] - 8 for message in messages]
    exponents = [message[head : head + 8, :128] for message, head in zip(messages, heads)]
    top = top_ref[...]
    for exponent in exponents:
        top = jnp.maximum(top, exponent)
    top = top + 2
    scale = jnp.exp2(-0.5 * top.astype(jnp.float32)) * TOP
    for j in range(WORDS // 128):
        cols = slice(128 * j, 128 * j + 128)
        for q in range(QUANTITIES):
            at = (l * QUANTITIES + q) * OWNED
            low = sums_ref[at : at + OWNED, cols]
            high = sums_ref[at : at + OWNED, 128 * j + WORDS : 128 * j + WORDS + 128]
            for message, head, exponent in zip(messages, heads, exponents):
                a, b = decode(message, at % head, exponent[q : q + 1, :], cols)
                low, high = low + a, high + b
            s = scale[q : q + 1, :]
            out_ref[q * OWNED : (q + 1) * OWNED, cols] = pack(encode(low, s), encode(high, s))
        out_ref[QUANTITIES * OWNED :, cols] = top


def combine(l, sums, top, messages):
    vmem = pl.BlockSpec(memory_space=pltpu.VMEM)
    return pl.pallas_call(
        functools.partial(combine_kernel, l),
        in_specs=[vmem] * (2 + len(messages)),
        out_specs=vmem,
        out_shape=jax.ShapeDtypeStruct((QUANTITIES * OWNED + 8, WORDS), jnp.int32),
        compiler_params=params(vmem_limit_bytes=16 * MB),
        cost_estimate=pl.CostEstimate(flops=2 * MB, bytes_accessed=2 * MB, transcendentals=0),
        name="combine",
    )(sums, top, *messages)


def finish_kernel(divisor_ref, sums_ref, message_ref, weighted_ref, linear_ref):
    inverse = 1.0 / divisor_ref[...]
    rows = QUANTITIES * OWNED
    exponents = message_ref[rows : rows + 8, :128]
    for j in range(WORDS // 128):
        cols = slice(128 * j, 128 * j + 128)
        pairs = [decode(message_ref, q * OWNED, exponents[q : q + 1, :], cols) for q in range(QUANTITIES)]
        for h in range(2):
            start = 128 * j + WORDS * h
            size = min(128, LAGS - start)
            linear, real, imag = [
                pairs[q][h] + sums_ref[q * OWNED : (q + 1) * OWNED, start : start + 128] for q in range(QUANTITIES)
            ]
            linear, real, imag = linear * inverse, real * inverse, imag * inverse
            weighted = linear * (real * real + imag * imag)
            linear_ref[:, start : start + size] = linear[:, :size]
            weighted_ref[:, start : start + size] = weighted[:, :size]


def finish(divisor, sums, message):
    vmem = pl.BlockSpec(memory_space=pltpu.VMEM)
    return pl.pallas_call(
        finish_kernel,
        in_specs=[vmem] * 3,
        out_specs=[vmem] * 2,
        out_shape=[jax.ShapeDtypeStruct((OWNED, LAGS), jnp.float32)] * 2,
        compiler_params=params(vmem_limit_bytes=16 * MB),
        name="finish",
    )(divisor, sums, message)


def shift(message, step, first):
    moves = []
    for x in range(SIDE):
        for y in range(SIDE):
            for pair in range(8):
                along_x = (pair % 2 == 0) == first
                to_x = (x + step) % SIDE if along_x else x
                to_y = y if along_x else (y + step) % SIDE
                moves.append(((x * SIDE + y) * 8 + pair, (to_x * SIDE + to_y) * 8 + pair))
    return lax.ppermute(message, ("day", "pair"), moves)


def trade(values, bit):
    moves = [(d * 8 + p, d * 8 + (p ^ bit)) for d in range(SIDE * SIDE) for p in range(8)]
    return lax.ppermute(values, ("day", "pair"), moves)


def stacks(correlations, mask, counts):
    place = (lax.axis_index("day") * 2 + lax.axis_index("pair") % 2).reshape(1)
    shifts = first_shifts()
    held, mask, stats, peak = energies(place, correlations, mask, shifts)
    others = trade(stats, 1)
    table = kernel_table(shifts)
    stats = add(stats, others)
    others = trade(stats, 2)
    rows = ordered_rows(place, held, mask)
    stats = add(stats, others)
    others = trade(stats, 6)
    rows = ordered_rows(place, held, mask, rows)
    rows = rows.reshape(SIDE, SIDE * DAYS * OWNED, WIDTH)

    def wide_step(k, first=0, count=SIDE):
        piece = terms(k, first, count, rows, table, stats, others, peak)
        return shift(piece, k, True) if k else piece

    def narrow_step(l):
        piece = combine(l, sums, top, [ahead, behind[l // 2]])
        return shift(piece, l, False) if l else piece

    far = [wide_step(2, 0, 2), wide_step(2, 2, 2)]
    ahead = wide_step(1)
    behind = [wide_step(3, 0, 2), wide_step(3, 2, 2)]
    own = wide_step(0)
    sums, top = gather([[own], far], SIDE)
    last, near, far, own = [narrow_step(l) for l in (2, 1, 3, 0)]
    sums, top = gather([[own], [near], [far]], 1)
    divisor = jnp.broadcast_to(jnp.maximum(counts.astype(jnp.float32), 1.0)[:, None], (OWNED, 128))
    return tuple(finish(divisor, sums, last))


def solution(mesh):
    placed = (P("day", "pair", None), P("day", "pair"), P(("pair", "day")))
    return jax.shard_map(
        stacks,
        mesh=mesh,
        in_specs=placed,
        out_specs=(P(("pair", "day"), None), P(("pair", "day"), None)),
        check_vma=False,
    )
```

profile of v0, /device:TPU:28, one launch (start us, length us, event | category | flops | bytes accessed | tf_op | source)
XLA Modules:
  0.0 88.2 jit_solution(17045036321292187325)
XLA Ops:
  1.3 3.8 %energy.1 = (bf16[16,2048,128]{2,1,0:T(8,128)(2,1)S(1)}, s32[4,512]{1,0:T(4,128)S(1)}, f32[8,128]{1,0:T(8,128)S(1)}, f32[8,128]{1,0:T(8,128)S(1)}) custom-call(s32[1]{0:T(128)} %bitcast.place_ref, bf16[32016,128]{1,0:T(8,128)(2,1)} %bitcast.13, s32[4,512]{1,0:T(4,128)} %given_ref.1, f32[8,4096]{1,0:T(8,128)S(1)} %fusion.12.shifts_ref), custom_call_target="tpu_custom_call" | custom-call | tf_op jit(solution)/shard_map/energy/pallas_call | solution.py:130
  5.2 3.8 %rows.2.refs_0_ = bf16[16,4,32,2048]{3,2,1,0:T(8,128)(2,1)S(1)} custom-call(s32[1]{0:T(128)} %bitcast.place_ref, bf16[16,2048,128]{2,1,0:T(8,128)(2,1)S(1)} %get-tuple-element.9.held_ref, s32[4,512]{1,0:T(4,128)S(1)} %get-tuple-element.10.mask_ref), custom_call_target="tpu_custom_call" | custom-call | flops 4000000000 | bytes 8388608 | tf_op jit(solution)/shard_map/rows/pallas_call | solution.py:185
  9.0 2.0 %collective-permute-start.1 = (f32[8,128]{1,0:T(8,128)S(1)}, f32[8,128]{1,0:T(8,128)S(1)}, u32[]{:S(2)}, u32[]{:S(2)}) collective-permute-start(f32[8,128]{1,0:T(8,128)S(1)} %add.83.a_ref), channel_id=1, source_target_pairs={{0,2},{1,3},{2,0},{3,1},{4,6},{5,7},{6,4},{7,5},{8,10},{9,11},{10,... | collective-permute-start | bytes 12296 | tf_op jit(solution)/shard_map/ppermute | solution.py:433
  11.0 3.8 %rows.3 = bf16[16,4,32,2048]{3,2,1,0:T(8,128)(2,1)S(1)} custom-call(s32[1]{0:T(128)} %bitcast.place_ref, bf16[16,2048,128]{2,1,0:T(8,128)(2,1)S(1)} %get-tuple-element.9.held_ref, s32[4,512]{1,0:T(4,128)S(1)} %get-tuple-element.10.mask_ref, bf16[16,4,32,2048]{3,2,1,0:T(8,128)(2,1)S(1)} %rows.2.refs_0_), custom_call_target="tpu_custom_call", output_to_operand_aliasing={{}: (3, {})} | custom-call | flops 4000000000 | bytes 8388608 | tf_op jit(solution)/shard_map/rows/pallas_call | solution.py:185
  14.9 2.6 %collective-permute-start.2 = (f32[8,128]{1,0:T(8,128)S(1)}, f32[8,128]{1,0:T(8,128)S(1)}, u32[]{:S(2)}, u32[]{:S(2)}) collective-permute-start(f32[8,128]{1,0:T(8,128)S(1)} %add.84.stats_ref), channel_id=1, source_target_pairs={{0,6},{1,7},{2,4},{3,5},{4,2},{5,3},{6,0},{7,1},{8,14},{9,15},{10,... | collective-permute-start | bytes 12296 | tf_op jit(solution)/shard_map/ppermute | solution.py:433
  17.5 2.0 %table.1.table_ref = bf16[8,2048,256]{2,1,0:T(8,128)(2,1)S(1)} custom-call(f32[8,4096]{1,0:T(8,128)S(1)} %fusion.12.shifts_ref), custom_call_target="tpu_custom_call" | custom-call | flops 1000000000 | bytes 8388608 | tf_op jit(solution)/shard_map/table/pallas_call | solution.py:199
  19.8 7.2 %terms.9 = s32[392,1024]{1,0:T(8,128)S(1)} custom-call(bf16[4,512,2048]{2,1,0:T(8,128)(2,1)S(1)} %bitcast.7, bf16[8,2048,256]{2,1,0:T(8,128)(2,1)S(1)} %table.1.table_ref, f32[8,128]{1,0:T(8,128)S(1)} %add.84.stats_ref, f32[8,128]{1,0:T(8,128)S(1)} %collective-permute-done.2.others_ref, f32[8,128]{1,0:T(8,128)S(1)} %get-tuple-element.12.peak_ref), custom_call_target="tpu_custom_call" | custom-call | flops 4294967296 | bytes 12582912 | tf_op jit(solution)/shard_map/terms/pallas_call | solution.py:289
  27.0 1.3 %collective-permute-start.5 = (s32[392,1024]{1,0:T(8,128)S(1)}, s32[392,1024]{1,0:T(8,128)S(1)}, u32[]{:S(2)}, u32[]{:S(2)}) collective-permute-start(s32[392,1024]{1,0:T(8,128)S(1)} %terms.9), channel_id=1, source_target_pairs={{0,32},{1,9},{2,34},{3,11},{4,36},{5,13},{6,38},{7,15},{8,40},{9,1... | collective-permute-start | bytes 4816904 | tf_op jit(solution)/shard_map/ppermute | solution.py:428
  28.3 4.0 %terms.7 = s32[200,1024]{1,0:T(8,128)S(1)} custom-call(bf16[4,512,2048]{2,1,0:T(8,128)(2,1)S(1)} %bitcast.8, bf16[8,2048,256]{2,1,0:T(8,128)(2,1)S(1)} %table.1.table_ref, f32[8,128]{1,0:T(8,128)S(1)} %add.84.stats_ref, f32[8,128]{1,0:T(8,128)S(1)} %collective-permute-done.2.others_ref, f32[8,128]{1,0:T(8,128)S(1)} %get-tuple-element.12.peak_ref), custom_call_target="tpu_custom_call" | custom-call | flops 2147483648 | bytes 12582912 | tf_op jit(solution)/shard_map/terms/pallas_call | solution.py:289
  32.3 0.9 collective-permute-start.3
  33.2 4.0 %terms.8 = s32[200,1024]{1,0:T(8,128)S(1)} custom-call(bf16[4,512,2048]{2,1,0:T(8,128)(2,1)S(1)} %bitcast.9, bf16[8,2048,256]{2,1,0:T(8,128)(2,1)S(1)} %table.1.table_ref, f32[8,128]{1,0:T(8,128)S(1)} %add.84.stats_ref, f32[8,128]{1,0:T(8,128)S(1)} %collective-permute-done.2.others_ref, f32[8,128]{1,0:T(8,128)S(1)} %get-tuple-element.12.peak_ref), custom_call_target="tpu_custom_call" | custom-call | flops 2147483648 | bytes 12582912 | tf_op jit(solution)/shard_map/terms/pallas_call | solution.py:289
  37.2 3.0 %collective-permute-start.4 = (s32[200,1024]{1,0:T(8,128)S(1)}, s32[200,1024]{1,0:T(8,128)S(1)}, u32[]{:S(2)}, u32[]{:S(2)}) collective-permute-start(s32[200,1024]{1,0:T(8,128)S(1)} %terms.8), channel_id=1, source_target_pairs={{0,64},{1,17},{2,66},{3,19},{4,68},{5,21},{6,70},{7,23},{8,72},{9,... | collective-permute-start | bytes 2457608 | tf_op jit(solution)/shard_map/ppermute | solution.py:428
  40.2 4.0 %terms.10 = s32[200,1024]{1,0:T(8,128)S(1)} custom-call(bf16[4,512,2048]{2,1,0:T(8,128)(2,1)S(1)} %bitcast.10, bf16[8,2048,256]{2,1,0:T(8,128)(2,1)S(1)} %table.1.table_ref, f32[8,128]{1,0:T(8,128)S(1)} %add.84.stats_ref, f32[8,128]{1,0:T(8,128)S(1)} %collective-permute-done.2.others_ref, f32[8,128]{1,0:T(8,128)S(1)} %get-tuple-element.12.peak_ref), custom_call_target="tpu_custom_call" | custom-call | flops 2147483648 | bytes 12582912 | tf_op jit(solution)/shard_map/terms/pallas_call | solution.py:289
  44.2 0.9 %collective-permute-start.6 = (s32[200,1024]{1,0:T(8,128)S(1)}, s32[200,1024]{1,0:T(8,128)S(1)}, u32[]{:S(2)}, u32[]{:S(2)}) collective-permute-start(s32[200,1024]{1,0:T(8,128)S(1)} %terms.10), channel_id=1, source_target_pairs={{0,96},{1,25},{2,98},{3,27},{4,100},{5,29},{6,102},{7,31},{8,104},... | collective-permute-start | bytes 2457608 | tf_op jit(solution)/shard_map/ppermute | solution.py:428
  45.1 4.0 %terms.11 = s32[200,1024]{1,0:T(8,128)S(1)} custom-call(bf16[4,512,2048]{2,1,0:T(8,128)(2,1)S(1)} %bitcast.11, bf16[8,2048,256]{2,1,0:T(8,128)(2,1)S(1)} %table.1.table_ref, f32[8,128]{1,0:T(8,128)S(1)} %add.84.stats_ref, f32[8,128]{1,0:T(8,128)S(1)} %collective-permute-done.2.others_ref, f32[8,128]{1,0:T(8,128)S(1)} %get-tuple-element.12.peak_ref), custom_call_target="tpu_custom_call" | custom-call | flops 2147483648 | bytes 12582912 | tf_op jit(solution)/shard_map/terms/pallas_call | solution.py:289
  49.7 7.2 %terms.6.refs_0_ = s32[392,1024]{1,0:T(8,128)S(1)} custom-call(bf16[4,512,2048]{2,1,0:T(8,128)(2,1)S(1)} %bitcast.12, bf16[8,2048,256]{2,1,0:T(8,128)(2,1)S(1)} %table.1.table_ref, f32[8,128]{1,0:T(8,128)S(1)} %add.84.stats_ref, f32[8,128]{1,0:T(8,128)S(1)} %collective-permute-done.2.others_ref, f32[8,128]{1,0:T(8,128)S(1)} %get-tuple-element.12.peak_ref), custom_call_target="tpu_custom_call" | custom-call | flops 4294967296 | bytes 12582912 | tf_op jit(solution)/shard_map/terms/pallas_call | solution.py:289
  56.9 9.5 %collective-permute-done.4.refs_2_ = s32[200,1024]{1,0:T(8,128)S(1)} collective-permute-done((s32[200,1024]{1,0:T(8,128)S(1)}, s32[200,1024]{1,0:T(8,128)S(1)}, u32[]{:S(2)}, u32[]{:S(2)}) %collective-permute-start.4) | collective-permute-done | bytes 819232 | tf_op jit(solution)/shard_map/ppermute | solution.py:428
  66.4 1.4 %gather.2 = (f32[384,2048]{1,0:T(8,128)S(1)}, s32[8,128]{1,0:T(8,128)S(1)}) custom-call(s32[392,1024]{1,0:T(8,128)S(1)} %terms.6.refs_0_, s32[200,1024]{1,0:T(8,128)S(1)} %collective-permute-done.3.refs_1_, s32[200,1024]{1,0:T(8,128)S(1)} %collective-permute-done.4.refs_2_), custom_call_target="tpu_custom_call" | custom-call | flops 4194304 | bytes 2097152 | tf_op jit(solution)/shard_map/gather/pallas_call | solution.py:338
  68.5 3.4 %collective-permute-done.8.refs_1_ = s32[200,1024]{1,0:T(8,128)S(1)} collective-permute-done((s32[200,1024]{1,0:T(8,128)S(1)}, s32[200,1024]{1,0:T(8,128)S(1)}, u32[]{:S(2)}, u32[]{:S(2)}) %collective-permute-start.8) | collective-permute-done | bytes 819232 | tf_op jit(solution)/shard_map/ppermute | solution.py:428
  72.6 0.8 collective-permute-start.9
  74.0 1.0 %collective-permute-start.10 = (s32[104,1024]{1,0:T(8,128)S(1)}, s32[104,1024]{1,0:T(8,128)S(1)}, u32[]{:S(2)}, u32[]{:S(2)}) collective-permute-start(s32[104,1024]{1,0:T(8,128)S(1)} %combine.7), channel_id=1, source_target_pairs={{0,16},{1,65},{2,18},{3,67},{4,20},{5,69},{6,22},{7,71},{8,24},{9,... | collective-permute-start | bytes 1277960 | tf_op jit(solution)/shard_map/ppermute | solution.py:428
  75.6 1.1 %collective-permute-done.7.refs_1_ = s32[104,1024]{1,0:T(8,128)S(1)} collective-permute-done((s32[104,1024]{1,0:T(8,128)S(1)}, s32[104,1024]{1,0:T(8,128)S(1)}, u32[]{:S(2)}, u32[]{:S(2)}) %collective-permute-start.7) | collective-permute-done | bytes 426016 | tf_op jit(solution)/shard_map/ppermute | solution.py:428
  76.6 9.9 %collective-permute-done.9.refs_2_ = s32[104,1024]{1,0:T(8,128)S(1)} collective-permute-done((s32[104,1024]{1,0:T(8,128)S(1)}, s32[104,1024]{1,0:T(8,128)S(1)}, u32[]{:S(2)}, u32[]{:S(2)}) %collective-permute-start.9) | collective-permute-done | bytes 426016 | tf_op jit(solution)/shard_map/ppermute | solution.py:428
  87.2 1.0 %finish.1 = (f32[32,2001]{1,0:T(8,128)}, f32[32,2001]{1,0:T(8,128)}) custom-call(f32[32,128]{1,0:T(8,128)S(1)} %broadcast_in_dim.11.divisor_ref, f32[96,2048]{1,0:T(8,128)S(1)} %get-tuple-element.15.sums_ref, s32[104,1024]{1,0:T(8,128)S(1)} %collective-permute-done.10.message_ref), custom_call_target="tpu_custom_call" | custom-call | tf_op jit(solution)/shard_map/finish/pallas_call | solution.py:409
  (22 shorter events, 4.8 us)
Async XLA Ops:
  5.1 3.9 %collective-permute-start = (f32[8,128]{1,0:T(8,128)S(1)}, f32[8,128]{1,0:T(8,128)S(1)}, u32[]{:S(2)}, u32[]{:S(2)}) collective-permute-start(f32[8,128]{1,0:T(8,128)S(1)} %get-tuple-element.11.a_ref), channel_id=1, source_target_pairs={{0,1},{1,0},{2,3},{3,2},{4,5},{5,4},{6,7},{7,6},{8,9},{9,8},{10,11... | collective-permute-start | bytes 12296 | tf_op jit(solution)/shard_map/ppermute | solution.py:433
  9.0 5.8 %collective-permute-start.1 = (f32[8,128]{1,0:T(8,128)S(1)}, f32[8,128]{1,0:T(8,128)S(1)}, u32[]{:S(2)}, u32[]{:S(2)}) collective-permute-start(f32[8,128]{1,0:T(8,128)S(1)} %add.83.a_ref), channel_id=1, source_target_pairs={{0,2},{1,3},{2,0},{3,1},{4,6},{5,7},{6,4},{7,5},{8,10},{9,11},{10,... | collective-permute-start | bytes 12296 | tf_op jit(solution)/shard_map/ppermute | solution.py:433
  14.9 4.9 %collective-permute-start.2 = (f32[8,128]{1,0:T(8,128)S(1)}, f32[8,128]{1,0:T(8,128)S(1)}, u32[]{:S(2)}, u32[]{:S(2)}) collective-permute-start(f32[8,128]{1,0:T(8,128)S(1)} %add.84.stats_ref), channel_id=1, source_target_pairs={{0,6},{1,7},{2,4},{3,5},{4,2},{5,3},{6,0},{7,1},{8,14},{9,15},{10,... | collective-permute-start | bytes 12296 | tf_op jit(solution)/shard_map/ppermute | solution.py:433
  27.0 40.8 %collective-permute-start.5 = (s32[392,1024]{1,0:T(8,128)S(1)}, s32[392,1024]{1,0:T(8,128)S(1)}, u32[]{:S(2)}, u32[]{:S(2)}) collective-permute-start(s32[392,1024]{1,0:T(8,128)S(1)} %terms.9), channel_id=1, source_target_pairs={{0,32},{1,9},{2,34},{3,11},{4,36},{5,13},{6,38},{7,15},{8,40},{9,1... | collective-permute-start | bytes 4816904 | tf_op jit(solution)/shard_map/ppermute | solution.py:428
  32.3 24.6 %collective-permute-start.3 = (s32[200,1024]{1,0:T(8,128)S(1)}, s32[200,1024]{1,0:T(8,128)S(1)}, u32[]{:S(2)}, u32[]{:S(2)}) collective-permute-start(s32[200,1024]{1,0:T(8,128)S(1)} %terms.7), channel_id=1, source_target_pairs={{0,64},{1,17},{2,66},{3,19},{4,68},{5,21},{6,70},{7,23},{8,72},{9,... | collective-permute-start | bytes 2457608 | tf_op jit(solution)/shard_map/ppermute | solution.py:428
  37.2 29.3 %collective-permute-start.4 = (s32[200,1024]{1,0:T(8,128)S(1)}, s32[200,1024]{1,0:T(8,128)S(1)}, u32[]{:S(2)}, u32[]{:S(2)}) collective-permute-start(s32[200,1024]{1,0:T(8,128)S(1)} %terms.8), channel_id=1, source_target_pairs={{0,64},{1,17},{2,66},{3,19},{4,68},{5,21},{6,70},{7,23},{8,72},{9,... | collective-permute-start | bytes 2457608 | tf_op jit(solution)/shard_map/ppermute | solution.py:428
  44.2 23.6 %collective-permute-start.6 = (s32[200,1024]{1,0:T(8,128)S(1)}, s32[200,1024]{1,0:T(8,128)S(1)}, u32[]{:S(2)}, u32[]{:S(2)}) collective-permute-start(s32[200,1024]{1,0:T(8,128)S(1)} %terms.10), channel_id=1, source_target_pairs={{0,96},{1,25},{2,98},{3,27},{4,100},{5,29},{6,102},{7,31},{8,104},... | collective-permute-start | bytes 2457608 | tf_op jit(solution)/shard_map/ppermute | solution.py:428
  49.1 22.9 %collective-permute-start.8 = (s32[200,1024]{1,0:T(8,128)S(1)}, s32[200,1024]{1,0:T(8,128)S(1)}, u32[]{:S(2)}, u32[]{:S(2)}) collective-permute-start(s32[200,1024]{1,0:T(8,128)S(1)} %terms.11), channel_id=1, source_target_pairs={{0,96},{1,25},{2,98},{3,27},{4,100},{5,29},{6,102},{7,31},{8,104},... | collective-permute-start | bytes 2457608 | tf_op jit(solution)/shard_map/ppermute | solution.py:428
  67.8 7.2 %copy-start = (s32[32]{0:T(128)S(1)}, s32[32]{0:T(128)}, u32[]{:S(2)}) copy-start(s32[32]{0:T(128)} %param.5) | copy-start | bytes 388
  68.4 8.2 %collective-permute-start.7 = (s32[104,1024]{1,0:T(8,128)S(1)}, s32[104,1024]{1,0:T(8,128)S(1)}, u32[]{:S(2)}, u32[]{:S(2)}) collective-permute-start(s32[104,1024]{1,0:T(8,128)S(1)} %combine.5), channel_id=1, source_target_pairs={{0,8},{1,33},{2,10},{3,35},{4,12},{5,37},{6,14},{7,39},{8,16},{9,4... | collective-permute-start | bytes 1277960 | tf_op jit(solution)/shard_map/ppermute | solution.py:428
  72.6 14.0 %collective-permute-start.9 = (s32[104,1024]{1,0:T(8,128)S(1)}, s32[104,1024]{1,0:T(8,128)S(1)}, u32[]{:S(2)}, u32[]{:S(2)}) collective-permute-start(s32[104,1024]{1,0:T(8,128)S(1)} %combine.6), channel_id=1, source_target_pairs={{0,24},{1,97},{2,26},{3,99},{4,28},{5,101},{6,30},{7,103},{8,0},{9... | collective-permute-start | bytes 1277960 | tf_op jit(solution)/shard_map/ppermute | solution.py:428
  74.0 13.2 %collective-permute-start.10 = (s32[104,1024]{1,0:T(8,128)S(1)}, s32[104,1024]{1,0:T(8,128)S(1)}, u32[]{:S(2)}, u32[]{:S(2)}) collective-permute-start(s32[104,1024]{1,0:T(8,128)S(1)} %combine.7), channel_id=1, source_target_pairs={{0,16},{1,65},{2,18},{3,67},{4,20},{5,69},{6,22},{7,71},{8,24},{9,... | collective-permute-start | bytes 1277960 | tf_op jit(solution)/shard_map/ppermute | solution.py:428
where the time goes:
time: 89.2 us; the launch traced here: 88.2 us
  Pallas kernels  49.2 us (55%)
  waiting for transfers between devices  24.2 us (27%)
  starting transfers between devices  13.2 us (15%)
    pallas_call x6, Pallas kernels, terms(): pl.pallas_call(functools.partial(terms_kernel, k, first, count), in_specs...  30.5 us
    ppermute x8, waiting for transfers between devices, shift(): return lax.ppermute(message, ('day', 'pair'), moves)  23.9 us
    ppermute x8, starting transfers between devices, shift(): return lax.ppermute(message, ('day', 'pair'), moves)  8.53 us
    pallas_call x2, Pallas kernels, ordered_rows(): pl.pallas_call(functools.partial(rows_kernel, *tiles), in_specs=[pl.Block...  7.63 us
    ppermute x3, starting transfers between devices, trade(): return lax.ppermute(values, ('day', 'pair'), moves)  4.68 us
    pallas_call x1, Pallas kernels, energies(): pl.pallas_call(energy_kernel, in_specs=[pl.BlockSpec(memory_space=pltpu.S...  3.79 us
    pallas_call x4, Pallas kernels, combine(): pl.pallas_call(functools.partial(combine_kernel, l), in_specs=[vmem] * (2...  2.4 us
    pallas_call x2, Pallas kernels, gather(): pl.pallas_call(functools.partial(gather_kernel, [len(message) for message...  1.97 us
  transfers between devices with their start and end apart: 11, of which 5 were waited for; matrix products, arithmetic and copies ran while one was open for 0% of the time, Pallas kernels for 42%

commit v1 on v0

--- a/solution.py
+++ b/solution.py
@@ -39,8 +39,20 @@
     return low * jnp.abs(low), high * jnp.abs(high)
 
 
+def tag(word, exponent):
+    lane = lax.broadcasted_iota(jnp.int32, word.shape, 1)
+    return jnp.where(lane == 127, pack(word & 0xFFFF, exponent.astype(jnp.int32) + 32768), word)
+
+
+def tagged(message_ref, q):
+    word = message_ref[q * OWNED : q * OWNED + 8, WORDS - 128 :]
+    lane = lax.broadcasted_iota(jnp.int32, word.shape, 1)
+    high = lax.shift_right_logical(word, 16).astype(jnp.float32) - 32768.0
+    return jnp.max(jnp.where(lane == 127, high, -65536.0), axis=1, keepdims=True)[:1, :]
+
+
 def unit(exponent):
-    return jnp.exp2(exponent.astype(jnp.float32)) * (1.0 / (TOP * TOP))
+    return jnp.exp2(exponent) * (1.0 / (TOP * TOP))
 
 
 def first_shifts():
@@ -236,10 +248,6 @@
     ]
     powers = [jnp.ceil(jnp.log(jnp.maximum(v, 1e-30) * 1.001) * 1.4426951) for v in bounds]
     scale = [TOP * jnp.exp2(-0.5 * p) for p in powers]
-    row = lax.broadcasted_iota(jnp.int32, (8, 128), 0)
-    exponents = jnp.where(row == 0, powers[0], jnp.where(row == 1, powers[1], powers[2])).astype(jnp.int32)
-    for n in range(WORDS // 128):
-        out_ref[count * QUANTITIES * OWNED :, 128 * n : 128 * n + 128] = exponents
     weights = [weight[d : d + 1, :] for d in range(DAYS)]
     floor = 0.25 / (weight * weight)
     floors = [floor[d : d + 1, :] for d in range(DAYS)]
@@ -250,7 +258,7 @@
             rows_ref[k, base : base + count * DAYS * OWNED, :], table_ref[n], preferred_element_type=jnp.float32
         )
 
-    def finish_block(n, hilbert_ref):
+    def finish_block(n, hilbert_ref, tags=False):
         for l in range(count):
             codes = []
             for h in range(2):
@@ -268,7 +276,10 @@
                 codes.append([encode(v, scale[q]) for q, v in enumerate((linear, real, imag))])
             for q in range(QUANTITIES):
                 at = (l * QUANTITIES + q) * OWNED
-                out_ref[at : at + OWNED, pl.ds(pl.multiple_of(n * 128, 128), 128)] = pack(codes[0][q], codes[1][q])
+                word = pack(codes[0][q], codes[1][q])
+                if tags:
+                    word = tag(word, powers[q])
+                out_ref[at : at + OWNED, pl.ds(pl.multiple_of(n * 128, 128), 128)] = word
 
     def step(i, carry):
         product(2 * i + 1, odd_ref)
@@ -281,7 +292,7 @@
     lax.fori_loop(0, 3, step, 0)
     product(7, odd_ref)
     finish_block(6, even_ref)
-    finish_block(7, odd_ref)
+    finish_block(7, odd_ref, True)
 
 
 def terms(k, first, count, rows, table, *stats):
@@ -290,7 +301,7 @@
         functools.partial(terms_kernel, k, first, count),
         in_specs=[vmem] * 5,
         out_specs=vmem,
-        out_shape=jax.ShapeDtypeStruct((count * QUANTITIES * OWNED + 8, WORDS), jnp.int32),
+        out_shape=jax.ShapeDtypeStruct((count * QUANTITIES * OWNED, WORDS), jnp.int32),
         scratch_shapes=[pltpu.VMEM((count * DAYS * OWNED, 256), jnp.float32)] * 2,
         compiler_params=params(vmem_limit_bytes=24 * MB),
         cost_estimate=pl.CostEstimate(
@@ -309,22 +320,19 @@
 def gather_kernel(cuts, blocks, *refs):
     refs, (out_ref, top_ref) = list(refs[:-2]), refs[-2:]
     messages = [[refs.pop(0) for _ in range(cut)] for cut in cuts]
-    heads = [parts[0].shape[0] - 8 for parts in messages]
-    top = None
-    for parts, head in zip(messages, heads):
-        exponents = parts[0][head : head + 8, :128]
-        top = exponents if top is None else jnp.maximum(top, exponents)
-    top_ref[...] = top
+    exponents = [[tagged(parts[0], q) for q in range(QUANTITIES)] for parts in messages]
+    row = lax.broadcasted_iota(jnp.int32, (8, 128), 0)
+    top = [functools.reduce(jnp.maximum, [e[q] for e in exponents]) for q in range(QUANTITIES)]
+    top_ref[...] = jnp.where(row == 0, top[0], jnp.where(row == 1, top[1], top[2]))
     for l in range(blocks):
         for j in range(WORDS // 128):
             cols = slice(128 * j, 128 * j + 128)
             for q in range(QUANTITIES):
                 low = high = None
-                for parts, head in zip(messages, heads):
+                for parts, exponent in zip(messages, exponents):
                     each = blocks // len(parts)
                     at = (l % each * QUANTITIES + q) * OWNED
-                    exponent = parts[0][head + q : head + q + 1, :128]
-                    a, b = decode(parts[l // each], at, exponent, cols)
+                    a, b = decode(parts[l // each], at, exponent[q], cols)
                     low = a if low is None else low + a
                     high = b if high is None else high + b
                 at = (l * QUANTITIES + q) * OWNED
@@ -341,7 +349,7 @@
         out_specs=[vmem] * 2,
         out_shape=[
             jax.ShapeDtypeStruct((blocks * QUANTITIES * OWNED, WIDTH), jnp.float32),
-            jax.ShapeDtypeStruct((8, 128), jnp.int32),
+            jax.ShapeDtypeStruct((8, 128), jnp.float32),
         ],
         compiler_params=params(vmem_limit_bytes=16 * MB),
         cost_estimate=pl.CostEstimate(flops=blocks * MB, bytes_accessed=2 * MB, transcendentals=0),
@@ -351,25 +359,24 @@
 
 def combine_kernel(l, sums_ref, top_ref, *refs):
     messages, out_ref = refs[:-1], refs[-1]
-    heads = [message.shape[0] - 8 for message in messages]
-    exponents = [message[head : head + 8, :128] for message, head in zip(messages, heads)]
-    top = top_ref[...]
-    for exponent in exponents:
-        top = jnp.maximum(top, exponent)
-    top = top + 2
-    scale = jnp.exp2(-0.5 * top.astype(jnp.float32)) * TOP
+    exponents = [[tagged(message, q) for q in range(QUANTITIES)] for message in messages]
+    tops = []
+    for q in range(QUANTITIES):
+        tops.append(functools.reduce(jnp.maximum, [e[q] for e in exponents], top_ref[q : q + 1, :]) + 2.0)
+    scale = [jnp.exp2(-0.5 * top) * TOP for top in tops]
     for j in range(WORDS // 128):
         cols = slice(128 * j, 128 * j + 128)
         for q in range(QUANTITIES):
             at = (l * QUANTITIES + q) * OWNED
             low = sums_ref[at : at + OWNED, cols]
             high = sums_ref[at : at + OWNED, 128 * j + WORDS : 128 * j + WORDS + 128]
-            for message, head, exponent in zip(messages, heads, exponents):
-                a, b = decode(message, at % head, exponent[q : q + 1, :], cols)
+            for message, exponent in zip(messages, exponents):
+                a, b = decode(message, at % message.shape[0], exponent[q], cols)
                 low, high = low + a, high + b
-            s = scale[q : q + 1, :]
-            out_ref[q * OWNED : (q + 1) * OWNED, cols] = pack(encode(low, s), encode(high, s))
-        out_ref[QUANTITIES * OWNED :, cols] = top
+            word = pack(encode(low, scale[q]), encode(high, scale[q]))
+            if j == WORDS // 128 - 1:
+                word = tag(word, tops[q])
+            out_ref[q * OWNED : (q + 1) * OWNED, cols] = word
 
 
 def combine(l, sums, top, messages):
@@ -378,7 +385,7 @@
         functools.partial(combine_kernel, l),
         in_specs=[vmem] * (2 + len(messages)),
         out_specs=vmem,
-        out_shape=jax.ShapeDtypeStruct((QUANTITIES * OWNED + 8, WORDS), jnp.int32),
+        out_shape=jax.ShapeDtypeStruct((QUANTITIES * OWNED, WORDS), jnp.int32),
         compiler_params=params(vmem_limit_bytes=16 * MB),
         cost_estimate=pl.CostEstimate(flops=2 * MB, bytes_accessed=2 * MB, transcendentals=0),
         name="combine",
@@ -387,11 +394,10 @@
 
 def finish_kernel(divisor_ref, sums_ref, message_ref, weighted_ref, linear_ref):
     inverse = 1.0 / divisor_ref[...]
-    rows = QUANTITIES * OWNED
-    exponents = message_ref[rows : rows + 8, :128]
+    exponents = [tagged(message_ref, q) for q in range(QUANTITIES)]
     for j in range(WORDS // 128):
         cols = slice(128 * j, 128 * j + 128)
-        pairs = [decode(message_ref, q * OWNED, exponents[q : q + 1, :], cols) for q in range(QUANTITIES)]
+        pairs = [decode(message_ref, q * OWNED, exponents[q], cols) for q in range(QUANTITIES)]
         for h in range(2):
             start = 128 * j + WORDS * h
             size = min(128, LAGS - start)

time: 89.2 us -> 87.3 us (0.979)
  waiting for transfers between devices: 24.2 us -> 22.1 us
    ppermute x8, waiting for transfers between devices: 23.9 us -> 21.8 us  [shift(): return lax.ppermute(message, ('day', 'pair'), moves)]
  transfers between devices with their start and end apart: 11 -> 11, of which waited for: 5 -> 5; matrix products, arithmetic and copies ran while one was open for 0% -> 0% of each run, Pallas kernels for 42% -> 43%
where the time goes in v1:
time: 87.3 us; the launch traced here: 86.3 us
  Pallas kernels  49.4 us (57%)
  waiting for transfers between devices  22.1 us (25%)
  starting transfers between devices  13.2 us (15%)
    pallas_call x6, Pallas kernels, terms(): pl.pallas_call(functools.partial(terms_kernel, k, first, count), in_specs...  30.4 us
    ppermute x8, waiting for transfers between devices, shift(): return lax.ppermute(message, ('day', 'pair'), moves)  21.8 us
    ppermute x8, starting transfers between devices, shift(): return lax.ppermute(message, ('day', 'pair'), moves)  8.53 us
    pallas_call x2, Pallas kernels, ordered_rows(): pl.pallas_call(functools.partial(rows_kernel, *tiles), in_specs=[pl.Block...  7.63 us
    ppermute x3, starting transfers between devices, trade(): return lax.ppermute(values, ('day', 'pair'), moves)  4.68 us
    pallas_call x1, Pallas kernels, energies(): pl.pallas_call(energy_kernel, in_specs=[pl.BlockSpec(memory_space=pltpu.S...  3.79 us
    pallas_call x4, Pallas kernels, combine(): pl.pallas_call(functools.partial(combine_kernel, l), in_specs=[vmem] * (2...  2.54 us
    pallas_call x2, Pallas kernels, gather(): pl.pallas_call(functools.partial(gather_kernel, [len(message) for message...  2.03 us
  transfers between devices with their start and end apart: 11, of which 5 were waited for; matrix products, arithmetic and copies ran while one was open for 0% of the time, Pallas kernels for 43%

profile of v1, /device:TPU:28, one launch (start us, length us, event | category | flops | bytes accessed | tf_op | source)
XLA Modules:
  0.0 86.3 jit_solution(8497760098629885468)
XLA Ops:
  1.3 3.8 %energy.1 = (bf16[16,2048,128]{2,1,0:T(8,128)(2,1)S(1)}, s32[4,512]{1,0:T(4,128)S(1)}, f32[8,128]{1,0:T(8,128)S(1)}, f32[8,128]{1,0:T(8,128)S(1)}) custom-call(s32[1]{0:T(128)} %bitcast.place_ref, bf16[32016,128]{1,0:T(8,128)(2,1)} %bitcast.13, s32[4,512]{1,0:T(4,128)} %given_ref.1, f32[8,4096]{1,0:T(8,128)S(1)} %fusion.12.shifts_ref), custom_call_target="tpu_custom_call" | custom-call | tf_op jit(solution)/shard_map/energy/pallas_call | solution.py:142
  5.2 3.8 %rows.2.refs_0_ = bf16[16,4,32,2048]{3,2,1,0:T(8,128)(2,1)S(1)} custom-call(s32[1]{0:T(128)} %bitcast.place_ref, bf16[16,2048,128]{2,1,0:T(8,128)(2,1)S(1)} %get-tuple-element.9.held_ref, s32[4,512]{1,0:T(4,128)S(1)} %get-tuple-element.10.mask_ref), custom_call_target="tpu_custom_call" | custom-call | flops 4000000000 | bytes 8388608 | tf_op jit(solution)/shard_map/rows/pallas_call | solution.py:197
  9.0 2.0 %collective-permute-start.1 = (f32[8,128]{1,0:T(8,128)S(1)}, f32[8,128]{1,0:T(8,128)S(1)}, u32[]{:S(2)}, u32[]{:S(2)}) collective-permute-start(f32[8,128]{1,0:T(8,128)S(1)} %add.83.a_ref), channel_id=1, source_target_pairs={{0,2},{1,3},{2,0},{3,1},{4,6},{5,7},{6,4},{7,5},{8,10},{9,11},{10,... | collective-permute-start | bytes 12296 | tf_op jit(solution)/shard_map/ppermute | solution.py:439
  11.0 3.8 %rows.3 = bf16[16,4,32,2048]{3,2,1,0:T(8,128)(2,1)S(1)} custom-call(s32[1]{0:T(128)} %bitcast.place_ref, bf16[16,2048,128]{2,1,0:T(8,128)(2,1)S(1)} %get-tuple-element.9.held_ref, s32[4,512]{1,0:T(4,128)S(1)} %get-tuple-element.10.mask_ref, bf16[16,4,32,2048]{3,2,1,0:T(8,128)(2,1)S(1)} %rows.2.refs_0_), custom_call_target="tpu_custom_call", output_to_operand_aliasing={{}: (3, {})} | custom-call | flops 4000000000 | bytes 8388608 | tf_op jit(solution)/shard_map/rows/pallas_call | solution.py:197
  14.9 2.6 %collective-permute-start.2 = (f32[8,128]{1,0:T(8,128)S(1)}, f32[8,128]{1,0:T(8,128)S(1)}, u32[]{:S(2)}, u32[]{:S(2)}) collective-permute-start(f32[8,128]{1,0:T(8,128)S(1)} %add.84.stats_ref), channel_id=1, source_target_pairs={{0,6},{1,7},{2,4},{3,5},{4,2},{5,3},{6,0},{7,1},{8,14},{9,15},{10,... | collective-permute-start | bytes 12296 | tf_op jit(solution)/shard_map/ppermute | solution.py:439
  17.5 2.0 %table.1.table_ref = bf16[8,2048,256]{2,1,0:T(8,128)(2,1)S(1)} custom-call(f32[8,4096]{1,0:T(8,128)S(1)} %fusion.12.shifts_ref), custom_call_target="tpu_custom_call" | custom-call | flops 1000000000 | bytes 8388608 | tf_op jit(solution)/shard_map/table/pallas_call | solution.py:211
  19.8 7.2 %terms.9 = s32[384,1024]{1,0:T(8,128)S(1)} custom-call(bf16[4,512,2048]{2,1,0:T(8,128)(2,1)S(1)} %bitcast.7, bf16[8,2048,256]{2,1,0:T(8,128)(2,1)S(1)} %table.1.table_ref, f32[8,128]{1,0:T(8,128)S(1)} %add.84.stats_ref, f32[8,128]{1,0:T(8,128)S(1)} %collective-permute-done.2.others_ref, f32[8,128]{1,0:T(8,128)S(1)} %get-tuple-element.12.peak_ref), custom_call_target="tpu_custom_call" | custom-call | flops 4294967296 | bytes 12582912 | tf_op jit(solution)/shard_map/terms/pallas_call | solution.py:300
  27.0 1.3 %collective-permute-start.5 = (s32[384,1024]{1,0:T(8,128)S(1)}, s32[384,1024]{1,0:T(8,128)S(1)}, u32[]{:S(2)}, u32[]{:S(2)}) collective-permute-start(s32[384,1024]{1,0:T(8,128)S(1)} %terms.9), channel_id=1, source_target_pairs={{0,32},{1,9},{2,34},{3,11},{4,36},{5,13},{6,38},{7,15},{8,40},{9,1... | collective-permute-start | bytes 4718600 | tf_op jit(solution)/shard_map/ppermute | solution.py:434
  28.3 4.0 %terms.7 = s32[192,1024]{1,0:T(8,128)S(1)} custom-call(bf16[4,512,2048]{2,1,0:T(8,128)(2,1)S(1)} %bitcast.8, bf16[8,2048,256]{2,1,0:T(8,128)(2,1)S(1)} %table.1.table_ref, f32[8,128]{1,0:T(8,128)S(1)} %add.84.stats_ref, f32[8,128]{1,0:T(8,128)S(1)} %collective-permute-done.2.others_ref, f32[8,128]{1,0:T(8,128)S(1)} %get-tuple-element.12.peak_ref), custom_call_target="tpu_custom_call" | custom-call | flops 2147483648 | bytes 12582912 | tf_op jit(solution)/shard_map/terms/pallas_call | solution.py:300
  32.3 0.9 %collective-permute-start.3 = (s32[192,1024]{1,0:T(8,128)S(1)}, s32[192,1024]{1,0:T(8,128)S(1)}, u32[]{:S(2)}, u32[]{:S(2)}) collective-permute-start(s32[192,1024]{1,0:T(8,128)S(1)} %terms.7), channel_id=1, source_target_pairs={{0,64},{1,17},{2,66},{3,19},{4,68},{5,21},{6,70},{7,23},{8,72},{9,... | collective-permute-start | bytes 2359304 | tf_op jit(solution)/shard_map/ppermute | solution.py:434
  33.2 4.0 %terms.8 = s32[192,1024]{1,0:T(8,128)S(1)} custom-call(bf16[4,512,2048]{2,1,0:T(8,128)(2,1)S(1)} %bitcast.9, bf16[8,2048,256]{2,1,0:T(8,128)(2,1)S(1)} %table.1.table_ref, f32[8,128]{1,0:T(8,128)S(1)} %add.84.stats_ref, f32[8,128]{1,0:T(8,128)S(1)} %collective-permute-done.2.others_ref, f32[8,128]{1,0:T(8,128)S(1)} %get-tuple-element.12.peak_ref), custom_call_target="tpu_custom_call" | custom-call | flops 2147483648 | bytes 12582912 | tf_op jit(solution)/shard_map/terms/pallas_call | solution.py:300
  37.1 3.0 %collective-permute-start.4 = (s32[192,1024]{1,0:T(8,128)S(1)}, s32[192,1024]{1,0:T(8,128)S(1)}, u32[]{:S(2)}, u32[]{:S(2)}) collective-permute-start(s32[192,1024]{1,0:T(8,128)S(1)} %terms.8), channel_id=1, source_target_pairs={{0,64},{1,17},{2,66},{3,19},{4,68},{5,21},{6,70},{7,23},{8,72},{9,... | collective-permute-start | bytes 2359304 | tf_op jit(solution)/shard_map/ppermute | solution.py:434
  40.1 4.0 %terms.10 = s32[192,1024]{1,0:T(8,128)S(1)} custom-call(bf16[4,512,2048]{2,1,0:T(8,128)(2,1)S(1)} %bitcast.10, bf16[8,2048,256]{2,1,0:T(8,128)(2,1)S(1)} %table.1.table_ref, f32[8,128]{1,0:T(8,128)S(1)} %add.84.stats_ref, f32[8,128]{1,0:T(8,128)S(1)} %collective-permute-done.2.others_ref, f32[8,128]{1,0:T(8,128)S(1)} %get-tuple-element.12.peak_ref), custom_call_target="tpu_custom_call" | custom-call | flops 2147483648 | bytes 12582912 | tf_op jit(solution)/shard_map/terms/pallas_call | solution.py:300
  44.1 0.9 %collective-permute-start.6 = (s32[192,1024]{1,0:T(8,128)S(1)}, s32[192,1024]{1,0:T(8,128)S(1)}, u32[]{:S(2)}, u32[]{:S(2)}) collective-permute-start(s32[192,1024]{1,0:T(8,128)S(1)} %terms.10), channel_id=1, source_target_pairs={{0,96},{1,25},{2,98},{3,27},{4,100},{5,29},{6,102},{7,31},{8,104},... | collective-permute-start | bytes 2359304 | tf_op jit(solution)/shard_map/ppermute | solution.py:434
  45.0 4.0 %terms.11 = s32[192,1024]{1,0:T(8,128)S(1)} custom-call(bf16[4,512,2048]{2,1,0:T(8,128)(2,1)S(1)} %bitcast.11, bf16[8,2048,256]{2,1,0:T(8,128)(2,1)S(1)} %table.1.table_ref, f32[8,128]{1,0:T(8,128)S(1)} %add.84.stats_ref, f32[8,128]{1,0:T(8,128)S(1)} %collective-permute-done.2.others_ref, f32[8,128]{1,0:T(8,128)S(1)} %get-tuple-element.12.peak_ref), custom_call_target="tpu_custom_call" | custom-call | flops 2147483648 | bytes 12582912 | tf_op jit(solution)/shard_map/terms/pallas_call | solution.py:300
  49.6 7.2 %terms.6.refs_0_ = s32[384,1024]{1,0:T(8,128)S(1)} custom-call(bf16[4,512,2048]{2,1,0:T(8,128)(2,1)S(1)} %bitcast.12, bf16[8,2048,256]{2,1,0:T(8,128)(2,1)S(1)} %table.1.table_ref, f32[8,128]{1,0:T(8,128)S(1)} %add.84.stats_ref, f32[8,128]{1,0:T(8,128)S(1)} %collective-permute-done.2.others_ref, f32[8,128]{1,0:T(8,128)S(1)} %get-tuple-element.12.peak_ref), custom_call_target="tpu_custom_call" | custom-call | flops 4294967296 | bytes 12582912 | tf_op jit(solution)/shard_map/terms/pallas_call | solution.py:300
  56.9 8.5 %collective-permute-done.4.refs_2_ = s32[192,1024]{1,0:T(8,128)S(1)} collective-permute-done((s32[192,1024]{1,0:T(8,128)S(1)}, s32[192,1024]{1,0:T(8,128)S(1)}, u32[]{:S(2)}, u32[]{:S(2)}) %collective-permute-start.4) | collective-permute-done | bytes 786464 | tf_op jit(solution)/shard_map/ppermute | solution.py:434
  65.4 1.3 %gather.2 = (f32[384,2048]{1,0:T(8,128)S(1)}, f32[8,128]{1,0:T(8,128)S(1)}) custom-call(s32[384,1024]{1,0:T(8,128)S(1)} %terms.6.refs_0_, s32[192,1024]{1,0:T(8,128)S(1)} %collective-permute-done.3.refs_1_, s32[192,1024]{1,0:T(8,128)S(1)} %collective-permute-done.4.refs_2_), custom_call_target="tpu_custom_call" | custom-call | flops 4194304 | bytes 2097152 | tf_op jit(solution)/shard_map/gather/pallas_call | solution.py:346
  67.5 3.1 %collective-permute-done.8.refs_1_ = s32[192,1024]{1,0:T(8,128)S(1)} collective-permute-done((s32[192,1024]{1,0:T(8,128)S(1)}, s32[192,1024]{1,0:T(8,128)S(1)}, u32[]{:S(2)}, u32[]{:S(2)}) %collective-permute-start.8) | collective-permute-done | bytes 786464 | tf_op jit(solution)/shard_map/ppermute | solution.py:434
  71.2 0.8 collective-permute-start.9
  72.6 1.0 %collective-permute-start.10 = (s32[96,1024]{1,0:T(8,128)S(1)}, s32[96,1024]{1,0:T(8,128)S(1)}, u32[]{:S(2)}, u32[]{:S(2)}) collective-permute-start(s32[96,1024]{1,0:T(8,128)S(1)} %combine.7), channel_id=1, source_target_pairs={{0,16},{1,65},{2,18},{3,67},{4,20},{5,69},{6,22},{7,71},{8,24},{9,... | collective-permute-start | bytes 1179656 | tf_op jit(solution)/shard_map/ppermute | solution.py:434
  74.3 1.0 %collective-permute-done.7.refs_1_ = s32[96,1024]{1,0:T(8,128)S(1)} collective-permute-done((s32[96,1024]{1,0:T(8,128)S(1)}, s32[96,1024]{1,0:T(8,128)S(1)}, u32[]{:S(2)}, u32[]{:S(2)}) %collective-permute-start.7) | collective-permute-done | bytes 393248 | tf_op jit(solution)/shard_map/ppermute | solution.py:434
  75.2 9.2 %collective-permute-done.9.refs_2_ = s32[96,1024]{1,0:T(8,128)S(1)} collective-permute-done((s32[96,1024]{1,0:T(8,128)S(1)}, s32[96,1024]{1,0:T(8,128)S(1)}, u32[]{:S(2)}, u32[]{:S(2)}) %collective-permute-start.9) | collective-permute-done | bytes 393248 | tf_op jit(solution)/shard_map/ppermute | solution.py:434
  85.2 1.1 %finish.1 = (f32[32,2001]{1,0:T(8,128)}, f32[32,2001]{1,0:T(8,128)}) custom-call(f32[32,128]{1,0:T(8,128)S(1)} %broadcast_in_dim.11.divisor_ref, f32[96,2048]{1,0:T(8,128)S(1)} %get-tuple-element.15.sums_ref, s32[96,1024]{1,0:T(8,128)S(1)} %collective-permute-done.10.message_ref), custom_call_target="tpu_custom_call" | custom-call | tf_op jit(solution)/shard_map/finish/pallas_call | solution.py:415
  (22 shorter events, 5.0 us)
Async XLA Ops:
  5.1 3.9 %collective-permute-start = (f32[8,128]{1,0:T(8,128)S(1)}, f32[8,128]{1,0:T(8,128)S(1)}, u32[]{:S(2)}, u32[]{:S(2)}) collective-permute-start(f32[8,128]{1,0:T(8,128)S(1)} %get-tuple-element.11.a_ref), channel_id=1, source_target_pairs={{0,1},{1,0},{2,3},{3,2},{4,5},{5,4},{6,7},{7,6},{8,9},{9,8},{10,11... | collective-permute-start | bytes 12296 | tf_op jit(solution)/shard_map/ppermute | solution.py:439
  9.0 5.8 %collective-permute-start.1 = (f32[8,128]{1,0:T(8,128)S(1)}, f32[8,128]{1,0:T(8,128)S(1)}, u32[]{:S(2)}, u32[]{:S(2)}) collective-permute-start(f32[8,128]{1,0:T(8,128)S(1)} %add.83.a_ref), channel_id=1, source_target_pairs={{0,2},{1,3},{2,0},{3,1},{4,6},{5,7},{6,4},{7,5},{8,10},{9,11},{10,... | collective-permute-start | bytes 12296 | tf_op jit(solution)/shard_map/ppermute | solution.py:439
  14.9 4.9 %collective-permute-start.2 = (f32[8,128]{1,0:T(8,128)S(1)}, f32[8,128]{1,0:T(8,128)S(1)}, u32[]{:S(2)}, u32[]{:S(2)}) collective-permute-start(f32[8,128]{1,0:T(8,128)S(1)} %add.84.stats_ref), channel_id=1, source_target_pairs={{0,6},{1,7},{2,4},{3,5},{4,2},{5,3},{6,0},{7,1},{8,14},{9,15},{10,... | collective-permute-start | bytes 12296 | tf_op jit(solution)/shard_map/ppermute | solution.py:439
  27.0 39.7 %collective-permute-start.5 = (s32[384,1024]{1,0:T(8,128)S(1)}, s32[384,1024]{1,0:T(8,128)S(1)}, u32[]{:S(2)}, u32[]{:S(2)}) collective-permute-start(s32[384,1024]{1,0:T(8,128)S(1)} %terms.9), channel_id=1, source_target_pairs={{0,32},{1,9},{2,34},{3,11},{4,36},{5,13},{6,38},{7,15},{8,40},{9,1... | collective-permute-start | bytes 4718600 | tf_op jit(solution)/shard_map/ppermute | solution.py:434
  32.3 24.6 %collective-permute-start.3 = (s32[192,1024]{1,0:T(8,128)S(1)}, s32[192,1024]{1,0:T(8,128)S(1)}, u32[]{:S(2)}, u32[]{:S(2)}) collective-permute-start(s32[192,1024]{1,0:T(8,128)S(1)} %terms.7), channel_id=1, source_target_pairs={{0,64},{1,17},{2,66},{3,19},{4,68},{5,21},{6,70},{7,23},{8,72},{9,... | collective-permute-start | bytes 2359304 | tf_op jit(solution)/shard_map/ppermute | solution.py:434
  37.1 28.2 %collective-permute-start.4 = (s32[192,1024]{1,0:T(8,128)S(1)}, s32[192,1024]{1,0:T(8,128)S(1)}, u32[]{:S(2)}, u32[]{:S(2)}) collective-permute-start(s32[192,1024]{1,0:T(8,128)S(1)} %terms.8), channel_id=1, source_target_pairs={{0,64},{1,17},{2,66},{3,19},{4,68},{5,21},{6,70},{7,23},{8,72},{9,... | collective-permute-start | bytes 2359304 | tf_op jit(solution)/shard_map/ppermute | solution.py:434
  44.1 22.6 %collective-permute-start.6 = (s32[192,1024]{1,0:T(8,128)S(1)}, s32[192,1024]{1,0:T(8,128)S(1)}, u32[]{:S(2)}, u32[]{:S(2)}) collective-permute-start(s32[192,1024]{1,0:T(8,128)S(1)} %terms.10), channel_id=1, source_target_pairs={{0,96},{1,25},{2,98},{3,27},{4,100},{5,29},{6,102},{7,31},{8,104},... | collective-permute-start | bytes 2359304 | tf_op jit(solution)/shard_map/ppermute | solution.py:434
  49.0 21.5 %collective-permute-start.8 = (s32[192,1024]{1,0:T(8,128)S(1)}, s32[192,1024]{1,0:T(8,128)S(1)}, u32[]{:S(2)}, u32[]{:S(2)}) collective-permute-start(s32[192,1024]{1,0:T(8,128)S(1)} %terms.11), channel_id=1, source_target_pairs={{0,96},{1,25},{2,98},{3,27},{4,100},{5,29},{6,102},{7,31},{8,104},... | collective-permute-start | bytes 2359304 | tf_op jit(solution)/shard_map/ppermute | solution.py:434
  66.7 6.9 %copy-start = (s32[32]{0:T(128)S(1)}, s32[32]{0:T(128)}, u32[]{:S(2)}) copy-start(s32[32]{0:T(128)} %param.5) | copy-start | bytes 388
  67.4 7.8 %collective-permute-start.7 = (s32[96,1024]{1,0:T(8,128)S(1)}, s32[96,1024]{1,0:T(8,128)S(1)}, u32[]{:S(2)}, u32[]{:S(2)}) collective-permute-start(s32[96,1024]{1,0:T(8,128)S(1)} %combine.5), channel_id=1, source_target_pairs={{0,8},{1,33},{2,10},{3,35},{4,12},{5,37},{6,14},{7,39},{8,16},{9,4... | collective-permute-start | bytes 1179656 | tf_op jit(solution)/shard_map/ppermute | solution.py:434
  71.2 13.3 %collective-permute-start.9 = (s32[96,1024]{1,0:T(8,128)S(1)}, s32[96,1024]{1,0:T(8,128)S(1)}, u32[]{:S(2)}, u32[]{:S(2)}) collective-permute-start(s32[96,1024]{1,0:T(8,128)S(1)} %combine.6), channel_id=1, source_target_pairs={{0,24},{1,97},{2,26},{3,99},{4,28},{5,101},{6,30},{7,103},{8,0},{9... | collective-permute-start | bytes 1179656 | tf_op jit(solution)/shard_map/ppermute | solution.py:434
  72.6 12.5 %collective-permute-start.10 = (s32[96,1024]{1,0:T(8,128)S(1)}, s32[96,1024]{1,0:T(8,128)S(1)}, u32[]{:S(2)}, u32[]{:S(2)}) collective-permute-start(s32[96,1024]{1,0:T(8,128)S(1)} %combine.7), channel_id=1, source_target_pairs={{0,16},{1,65},{2,18},{3,67},{4,20},{5,69},{6,22},{7,71},{8,24},{9,... | collective-permute-start | bytes 1179656 | tf_op jit(solution)/shard_map/ppermute | solution.py:434

commit v2 on v1

--- a/solution.py
+++ b/solution.py
@@ -392,12 +392,16 @@
     )(sums, top, *messages)
 
 
-def finish_kernel(divisor_ref, sums_ref, message_ref, weighted_ref, linear_ref):
+def finish_kernel(divisor_ref, sums_ref, *refs):
+    messages, (weighted_ref, linear_ref) = refs[:-2], refs[-2:]
     inverse = 1.0 / divisor_ref[...]
-    exponents = [tagged(message_ref, q) for q in range(QUANTITIES)]
+    exponents = [[tagged(message, q) for q in range(QUANTITIES)] for message in messages]
     for j in range(WORDS // 128):
         cols = slice(128 * j, 128 * j + 128)
-        pairs = [decode(message_ref, q * OWNED, exponents[q], cols) for q in range(QUANTITIES)]
+        pairs = []
+        for q in range(QUANTITIES):
+            both = [decode(message, q * OWNED, e[q], cols) for message, e in zip(messages, exponents)]
+            pairs.append([sum(each[1:], each[0]) for each in zip(*both)])
         for h in range(2):
             start = 128 * j + WORDS * h
             size = min(128, LAGS - start)
@@ -410,16 +414,16 @@
             weighted_ref[:, start : start + size] = weighted[:, :size]
 
 
-def finish(divisor, sums, message):
+def finish(divisor, sums, messages):
     vmem = pl.BlockSpec(memory_space=pltpu.VMEM)
     return pl.pallas_call(
         finish_kernel,
-        in_specs=[vmem] * 3,
+        in_specs=[vmem] * (2 + len(messages)),
         out_specs=[vmem] * 2,
         out_shape=[jax.ShapeDtypeStruct((OWNED, LAGS), jnp.float32)] * 2,
         compiler_params=params(vmem_limit_bytes=16 * MB),
         name="finish",
-    )(divisor, sums, message)
+    )(divisor, sums, *messages)
 
 
 def shift(message, step, first):
@@ -467,9 +471,9 @@
     own = wide_step(0)
     sums, top = gather([[own], far], SIDE)
     last, near, far, own = [narrow_step(l) for l in (2, 1, 3, 0)]
-    sums, top = gather([[own], [near], [far]], 1)
+    sums, top = gather([[own], [last]], 1)
     divisor = jnp.broadcast_to(jnp.maximum(counts.astype(jnp.float32), 1.0)[:, None], (OWNED, 128))
-    return tuple(finish(divisor, sums, last))
+    return tuple(finish(divisor, sums, [near, far]))
 
 
 def solution(mesh):

time: 87.3 us -> 88.9 us (1.018)
  the two profiles are of different devices: /device:TPU:28 before, /device:TPU:18 now
where the time goes in v2:
time: 88.9 us; the launch traced here: 88.8 us
  Pallas kernels  49.6 us (56%)
  waiting for transfers between devices  20.1 us (23%)
  starting transfers between devices  17.6 us (20%)
    pallas_call x6, Pallas kernels, terms(): pl.pallas_call(functools.partial(terms_kernel, k, first, count), in_specs...  30.4 us
    ppermute x8, waiting for transfers between devices, shift(): return lax.ppermute(message, ('day', 'pair'), moves)  19.8 us
    ppermute x8, starting transfers between devices, shift(): return lax.ppermute(message, ('day', 'pair'), moves)  12.9 us
    pallas_call x2, Pallas kernels, ordered_rows(): pl.pallas_call(functools.partial(rows_kernel, *tiles), in_specs=[pl.Block...  7.61 us
    ppermute x3, starting transfers between devices, trade(): return lax.ppermute(values, ('day', 'pair'), moves)  4.69 us
    pallas_call x1, Pallas kernels, energies(): pl.pallas_call(energy_kernel, in_specs=[pl.BlockSpec(memory_space=pltpu.S...  3.79 us
    pallas_call x4, Pallas kernels, combine(): pl.pallas_call(functools.partial(combine_kernel, l), in_specs=[vmem] * (2...  2.54 us
    pallas_call x2, Pallas kernels, gather(): pl.pallas_call(functools.partial(gather_kernel, [len(message) for message...  2.03 us
  transfers between devices with their start and end apart: 11, of which 5 were waited for; matrix products, arithmetic and copies ran while one was open for 0% of the time, Pallas kernels for 42%

profile of v2, /device:TPU:18, one launch (start us, length us, event | category | flops | bytes accessed | tf_op | source)
XLA Modules:
  0.0 88.8 jit_solution(1677321743961880088)
XLA Ops:
  1.3 3.8 %energy.1 = (bf16[16,2048,128]{2,1,0:T(8,128)(2,1)S(1)}, s32[4,512]{1,0:T(4,128)S(1)}, f32[8,128]{1,0:T(8,128)S(1)}, f32[8,128]{1,0:T(8,128)S(1)}) custom-call(s32[1]{0:T(128)} %bitcast.place_ref, bf16[32016,128]{1,0:T(8,128)(2,1)} %bitcast.13, s32[4,512]{1,0:T(4,128)} %given_ref.1, f32[8,4096]{1,0:T(8,128)S(1)} %fusion.12.shifts_ref), custom_call_target="tpu_custom_call" | custom-call | tf_op jit(solution)/shard_map/energy/pallas_call | solution.py:142
  5.2 3.8 %rows.2.refs_0_ = bf16[16,4,32,2048]{3,2,1,0:T(8,128)(2,1)S(1)} custom-call(s32[1]{0:T(128)} %bitcast.place_ref, bf16[16,2048,128]{2,1,0:T(8,128)(2,1)S(1)} %get-tuple-element.9.held_ref, s32[4,512]{1,0:T(4,128)S(1)} %get-tuple-element.10.mask_ref), custom_call_target="tpu_custom_call" | custom-call | flops 4000000000 | bytes 8388608 | tf_op jit(solution)/shard_map/rows/pallas_call | solution.py:197
  9.0 2.0 %collective-permute-start.1 = (f32[8,128]{1,0:T(8,128)S(1)}, f32[8,128]{1,0:T(8,128)S(1)}, u32[]{:S(2)}, u32[]{:S(2)}) collective-permute-start(f32[8,128]{1,0:T(8,128)S(1)} %add.83.a_ref), channel_id=1, source_target_pairs={{0,2},{1,3},{2,0},{3,1},{4,6},{5,7},{6,4},{7,5},{8,10},{9,11},{10,... | collective-permute-start | bytes 12296 | tf_op jit(solution)/shard_map/ppermute | solution.py:443
  11.0 3.8 %rows.3 = bf16[16,4,32,2048]{3,2,1,0:T(8,128)(2,1)S(1)} custom-call(s32[1]{0:T(128)} %bitcast.place_ref, bf16[16,2048,128]{2,1,0:T(8,128)(2,1)S(1)} %get-tuple-element.9.held_ref, s32[4,512]{1,0:T(4,128)S(1)} %get-tuple-element.10.mask_ref, bf16[16,4,32,2048]{3,2,1,0:T(8,128)(2,1)S(1)} %rows.2.refs_0_), custom_call_target="tpu_custom_call", output_to_operand_aliasing={{}: (3, {})} | custom-call | flops 4000000000 | bytes 8388608 | tf_op jit(solution)/shard_map/rows/pallas_call | solution.py:197
  14.9 2.6 %collective-permute-start.2 = (f32[8,128]{1,0:T(8,128)S(1)}, f32[8,128]{1,0:T(8,128)S(1)}, u32[]{:S(2)}, u32[]{:S(2)}) collective-permute-start(f32[8,128]{1,0:T(8,128)S(1)} %add.84.stats_ref), channel_id=1, source_target_pairs={{0,6},{1,7},{2,4},{3,5},{4,2},{5,3},{6,0},{7,1},{8,14},{9,15},{10,... | collective-permute-start | bytes 12296 | tf_op jit(solution)/shard_map/ppermute | solution.py:443
  17.5 2.0 %table.1.table_ref = bf16[8,2048,256]{2,1,0:T(8,128)(2,1)S(1)} custom-call(f32[8,4096]{1,0:T(8,128)S(1)} %fusion.12.shifts_ref), custom_call_target="tpu_custom_call" | custom-call | flops 1000000000 | bytes 8388608 | tf_op jit(solution)/shard_map/table/pallas_call | solution.py:211
  19.8 7.2 %terms.9 = s32[384,1024]{1,0:T(8,128)S(1)} custom-call(bf16[4,512,2048]{2,1,0:T(8,128)(2,1)S(1)} %bitcast.7, bf16[8,2048,256]{2,1,0:T(8,128)(2,1)S(1)} %table.1.table_ref, f32[8,128]{1,0:T(8,128)S(1)} %add.84.stats_ref, f32[8,128]{1,0:T(8,128)S(1)} %collective-permute-done.2.others_ref, f32[8,128]{1,0:T(8,128)S(1)} %get-tuple-element.12.peak_ref), custom_call_target="tpu_custom_call" | custom-call | flops 4294967296 | bytes 12582912 | tf_op jit(solution)/shard_map/terms/pallas_call | solution.py:300
  27.0 1.6 %collective-permute-start.5 = (s32[384,1024]{1,0:T(8,128)S(1)}, s32[384,1024]{1,0:T(8,128)S(1)}, u32[]{:S(2)}, u32[]{:S(2)}) collective-permute-start(s32[384,1024]{1,0:T(8,128)S(1)} %terms.9), channel_id=1, source_target_pairs={{0,32},{1,9},{2,34},{3,11},{4,36},{5,13},{6,38},{7,15},{8,40},{9,1... | collective-permute-start | bytes 4718600 | tf_op jit(solution)/shard_map/ppermute | solution.py:438
  28.6 4.0 %terms.7 = s32[192,1024]{1,0:T(8,128)S(1)} custom-call(bf16[4,512,2048]{2,1,0:T(8,128)(2,1)S(1)} %bitcast.8, bf16[8,2048,256]{2,1,0:T(8,128)(2,1)S(1)} %table.1.table_ref, f32[8,128]{1,0:T(8,128)S(1)} %add.84.stats_ref, f32[8,128]{1,0:T(8,128)S(1)} %collective-permute-done.2.others_ref, f32[8,128]{1,0:T(8,128)S(1)} %get-tuple-element.12.peak_ref), custom_call_target="tpu_custom_call" | custom-call | flops 2147483648 | bytes 12582912 | tf_op jit(solution)/shard_map/terms/pallas_call | solution.py:300
  32.6 1.2 %collective-permute-start.3 = (s32[192,1024]{1,0:T(8,128)S(1)}, s32[192,1024]{1,0:T(8,128)S(1)}, u32[]{:S(2)}, u32[]{:S(2)}) collective-permute-start(s32[192,1024]{1,0:T(8,128)S(1)} %terms.7), channel_id=1, source_target_pairs={{0,64},{1,17},{2,66},{3,19},{4,68},{5,21},{6,70},{7,23},{8,72},{9,... | collective-permute-start | bytes 2359304 | tf_op jit(solution)/shard_map/ppermute | solution.py:438
  33.7 4.0 %terms.8 = s32[192,1024]{1,0:T(8,128)S(1)} custom-call(bf16[4,512,2048]{2,1,0:T(8,128)(2,1)S(1)} %bitcast.9, bf16[8,2048,256]{2,1,0:T(8,128)(2,1)S(1)} %table.1.table_ref, f32[8,128]{1,0:T(8,128)S(1)} %add.84.stats_ref, f32[8,128]{1,0:T(8,128)S(1)} %collective-permute-done.2.others_ref, f32[8,128]{1,0:T(8,128)S(1)} %get-tuple-element.12.peak_ref), custom_call_target="tpu_custom_call" | custom-call | flops 2147483648 | bytes 12582912 | tf_op jit(solution)/shard_map/terms/pallas_call | solution.py:300
  37.7 2.7 %collective-permute-start.4 = (s32[192,1024]{1,0:T(8,128)S(1)}, s32[192,1024]{1,0:T(8,128)S(1)}, u32[]{:S(2)}, u32[]{:S(2)}) collective-permute-start(s32[192,1024]{1,0:T(8,128)S(1)} %terms.8), channel_id=1, source_target_pairs={{0,64},{1,17},{2,66},{3,19},{4,68},{5,21},{6,70},{7,23},{8,72},{9,... | collective-permute-start | bytes 2359304 | tf_op jit(solution)/shard_map/ppermute | solution.py:438
  40.4 4.0 %terms.11 = s32[192,1024]{1,0:T(8,128)S(1)} custom-call(bf16[4,512,2048]{2,1,0:T(8,128)(2,1)S(1)} %bitcast.10, bf16[8,2048,256]{2,1,0:T(8,128)(2,1)S(1)} %table.1.table_ref, f32[8,128]{1,0:T(8,128)S(1)} %add.84.stats_ref, f32[8,128]{1,0:T(8,128)S(1)} %collective-permute-done.2.others_ref, f32[8,128]{1,0:T(8,128)S(1)} %get-tuple-element.12.peak_ref), custom_call_target="tpu_custom_call" | custom-call | flops 2147483648 | bytes 12582912 | tf_op jit(solution)/shard_map/terms/pallas_call | solution.py:300
  45.0 4.0 %terms.10 = s32[192,1024]{1,0:T(8,128)S(1)} custom-call(bf16[4,512,2048]{2,1,0:T(8,128)(2,1)S(1)} %bitcast.11, bf16[8,2048,256]{2,1,0:T(8,128)(2,1)S(1)} %table.1.table_ref, f32[8,128]{1,0:T(8,128)S(1)} %add.84.stats_ref, f32[8,128]{1,0:T(8,128)S(1)} %collective-permute-done.2.others_ref, f32[8,128]{1,0:T(8,128)S(1)} %get-tuple-element.12.peak_ref), custom_call_target="tpu_custom_call" | custom-call | flops 2147483648 | bytes 12582912 | tf_op jit(solution)/shard_map/terms/pallas_call | solution.py:300
  49.0 1.8 %collective-permute-start.6 = (s32[192,1024]{1,0:T(8,128)S(1)}, s32[192,1024]{1,0:T(8,128)S(1)}, u32[]{:S(2)}, u32[]{:S(2)}) collective-permute-start(s32[192,1024]{1,0:T(8,128)S(1)} %terms.10), channel_id=1, source_target_pairs={{0,96},{1,25},{2,98},{3,27},{4,100},{5,29},{6,102},{7,31},{8,104},... | collective-permute-start | bytes 2359304 | tf_op jit(solution)/shard_map/ppermute | solution.py:438
  50.8 7.2 %terms.6.refs_0_ = s32[384,1024]{1,0:T(8,128)S(1)} custom-call(bf16[4,512,2048]{2,1,0:T(8,128)(2,1)S(1)} %bitcast.12, bf16[8,2048,256]{2,1,0:T(8,128)(2,1)S(1)} %table.1.table_ref, f32[8,128]{1,0:T(8,128)S(1)} %add.84.stats_ref, f32[8,128]{1,0:T(8,128)S(1)} %collective-permute-done.2.others_ref, f32[8,128]{1,0:T(8,128)S(1)} %get-tuple-element.12.peak_ref), custom_call_target="tpu_custom_call" | custom-call | flops 4294967296 | bytes 12582912 | tf_op jit(solution)/shard_map/terms/pallas_call | solution.py:300
  58.1 1.3 %gather.2 = (f32[384,2048]{1,0:T(8,128)S(1)}, f32[8,128]{1,0:T(8,128)S(1)}) custom-call(s32[384,1024]{1,0:T(8,128)S(1)} %terms.6.refs_0_, s32[192,1024]{1,0:T(8,128)S(1)} %collective-permute-done.3.refs_1_, s32[192,1024]{1,0:T(8,128)S(1)} %collective-permute-done.4.refs_2_), custom_call_target="tpu_custom_call" | custom-call | flops 4194304 | bytes 2097152 | tf_op jit(solution)/shard_map/gather/pallas_call | solution.py:346
  59.4 3.6 %collective-permute-done.7.refs_1_ = s32[192,1024]{1,0:T(8,128)S(1)} collective-permute-done((s32[192,1024]{1,0:T(8,128)S(1)}, s32[192,1024]{1,0:T(8,128)S(1)}, u32[]{:S(2)}, u32[]{:S(2)}) %collective-permute-start.7) | collective-permute-done | bytes 786464 | tf_op jit(solution)/shard_map/ppermute | solution.py:438
  64.0 9.8 %collective-permute-done.6.refs_1_ = s32[192,1024]{1,0:T(8,128)S(1)} collective-permute-done((s32[192,1024]{1,0:T(8,128)S(1)}, s32[192,1024]{1,0:T(8,128)S(1)}, u32[]{:S(2)}, u32[]{:S(2)}) %collective-permute-start.6) | collective-permute-done | bytes 786464 | tf_op jit(solution)/shard_map/ppermute | solution.py:438
  74.5 4.6 %collective-permute-start.9 = (s32[96,1024]{1,0:T(8,128)S(1)}, s32[96,1024]{1,0:T(8,128)S(1)}, u32[]{:S(2)}, u32[]{:S(2)}) collective-permute-start(s32[96,1024]{1,0:T(8,128)S(1)} %combine.6), channel_id=1, source_target_pairs={{0,8},{1,33},{2,10},{3,35},{4,12},{5,37},{6,14},{7,39},{8,16},{9,4... | collective-permute-start | bytes 1179656 | tf_op jit(solution)/shard_map/ppermute | solution.py:438
  80.4 0.7 gather.3
  81.1 3.2 %collective-permute-done.9.refs_0_ = s32[96,1024]{1,0:T(8,128)S(1)} collective-permute-done((s32[96,1024]{1,0:T(8,128)S(1)}, s32[96,1024]{1,0:T(8,128)S(1)}, u32[]{:S(2)}, u32[]{:S(2)}) %collective-permute-start.9) | collective-permute-done | bytes 393248 | tf_op jit(solution)/shard_map/ppermute | solution.py:438
  84.3 3.2 %collective-permute-done.10.refs_1_ = s32[96,1024]{1,0:T(8,128)S(1)} collective-permute-done((s32[96,1024]{1,0:T(8,128)S(1)}, s32[96,1024]{1,0:T(8,128)S(1)}, u32[]{:S(2)}, u32[]{:S(2)}) %collective-permute-start.10) | collective-permute-done | bytes 393248 | tf_op jit(solution)/shard_map/ppermute | solution.py:438
  87.6 1.2 %finish.1 = (f32[32,2001]{1,0:T(8,128)}, f32[32,2001]{1,0:T(8,128)}) custom-call(f32[32,128]{1,0:T(8,128)S(1)} %broadcast_in_dim.11.divisor_ref, f32[96,2048]{1,0:T(8,128)S(1)} %get-tuple-element.15.sums_ref, s32[96,1024]{1,0:T(8,128)S(1)} %collective-permute-done.9.refs_0_, s32[96,1024]{1,0:T(8,128)S(1)} %collective-permute-done.10.refs_1_), custom_call_target="tpu_custom_call" | custom-call | tf_op jit(solution)/shard_map/finish/pallas_call | solution.py:419
  (22 shorter events, 4.8 us)
Async XLA Ops:
  5.1 3.9 %collective-permute-start = (f32[8,128]{1,0:T(8,128)S(1)}, f32[8,128]{1,0:T(8,128)S(1)}, u32[]{:S(2)}, u32[]{:S(2)}) collective-permute-start(f32[8,128]{1,0:T(8,128)S(1)} %get-tuple-element.11.a_ref), channel_id=1, source_target_pairs={{0,1},{1,0},{2,3},{3,2},{4,5},{5,4},{6,7},{7,6},{8,9},{9,8},{10,11... | collective-permute-start | bytes 12296 | tf_op jit(solution)/shard_map/ppermute | solution.py:443
  9.0 5.8 %collective-permute-start.1 = (f32[8,128]{1,0:T(8,128)S(1)}, f32[8,128]{1,0:T(8,128)S(1)}, u32[]{:S(2)}, u32[]{:S(2)}) collective-permute-start(f32[8,128]{1,0:T(8,128)S(1)} %add.83.a_ref), channel_id=1, source_target_pairs={{0,2},{1,3},{2,0},{3,1},{4,6},{5,7},{6,4},{7,5},{8,10},{9,11},{10,... | collective-permute-start | bytes 12296 | tf_op jit(solution)/shard_map/ppermute | solution.py:443
  14.9 4.9 %collective-permute-start.2 = (f32[8,128]{1,0:T(8,128)S(1)}, f32[8,128]{1,0:T(8,128)S(1)}, u32[]{:S(2)}, u32[]{:S(2)}) collective-permute-start(f32[8,128]{1,0:T(8,128)S(1)} %add.84.stats_ref), channel_id=1, source_target_pairs={{0,6},{1,7},{2,4},{3,5},{4,2},{5,3},{6,0},{7,1},{8,14},{9,15},{10,... | collective-permute-start | bytes 12296 | tf_op jit(solution)/shard_map/ppermute | solution.py:443
  27.0 36.0 %collective-permute-start.5 = (s32[384,1024]{1,0:T(8,128)S(1)}, s32[384,1024]{1,0:T(8,128)S(1)}, u32[]{:S(2)}, u32[]{:S(2)}) collective-permute-start(s32[384,1024]{1,0:T(8,128)S(1)} %terms.9), channel_id=1, source_target_pairs={{0,32},{1,9},{2,34},{3,11},{4,36},{5,13},{6,38},{7,15},{8,40},{9,1... | collective-permute-start | bytes 4718600 | tf_op jit(solution)/shard_map/ppermute | solution.py:438
  32.6 25.5 %collective-permute-start.3 = (s32[192,1024]{1,0:T(8,128)S(1)}, s32[192,1024]{1,0:T(8,128)S(1)}, u32[]{:S(2)}, u32[]{:S(2)}) collective-permute-start(s32[192,1024]{1,0:T(8,128)S(1)} %terms.7), channel_id=1, source_target_pairs={{0,64},{1,17},{2,66},{3,19},{4,68},{5,21},{6,70},{7,23},{8,72},{9,... | collective-permute-start | bytes 2359304 | tf_op jit(solution)/shard_map/ppermute | solution.py:438
  37.7 20.3 %collective-permute-start.4 = (s32[192,1024]{1,0:T(8,128)S(1)}, s32[192,1024]{1,0:T(8,128)S(1)}, u32[]{:S(2)}, u32[]{:S(2)}) collective-permute-start(s32[192,1024]{1,0:T(8,128)S(1)} %terms.8), channel_id=1, source_target_pairs={{0,64},{1,17},{2,66},{3,19},{4,68},{5,21},{6,70},{7,23},{8,72},{9,... | collective-permute-start | bytes 2359304 | tf_op jit(solution)/shard_map/ppermute | solution.py:438
  44.4 18.6 %collective-permute-start.7 = (s32[192,1024]{1,0:T(8,128)S(1)}, s32[192,1024]{1,0:T(8,128)S(1)}, u32[]{:S(2)}, u32[]{:S(2)}) collective-permute-start(s32[192,1024]{1,0:T(8,128)S(1)} %terms.11), channel_id=1, source_target_pairs={{0,96},{1,25},{2,98},{3,27},{4,100},{5,29},{6,102},{7,31},{8,104},... | collective-permute-start | bytes 2359304 | tf_op jit(solution)/shard_map/ppermute | solution.py:438
  49.0 24.8 %collective-permute-start.6 = (s32[192,1024]{1,0:T(8,128)S(1)}, s32[192,1024]{1,0:T(8,128)S(1)}, u32[]{:S(2)}, u32[]{:S(2)}) collective-permute-start(s32[192,1024]{1,0:T(8,128)S(1)} %terms.10), channel_id=1, source_target_pairs={{0,96},{1,25},{2,98},{3,27},{4,100},{5,29},{6,102},{7,31},{8,104},... | collective-permute-start | bytes 2359304 | tf_op jit(solution)/shard_map/ppermute | solution.py:438
  63.0 16.8 %copy-start = (s32[32]{0:T(128)S(1)}, s32[32]{0:T(128)}, u32[]{:S(2)}) copy-start(s32[32]{0:T(128)} %param.5) | copy-start | bytes 388
  63.6 16.8 %collective-permute-start.8 = (s32[96,1024]{1,0:T(8,128)S(1)}, s32[96,1024]{1,0:T(8,128)S(1)}, u32[]{:S(2)}, u32[]{:S(2)}) collective-permute-start(s32[96,1024]{1,0:T(8,128)S(1)} %combine.5), channel_id=1, source_target_pairs={{0,16},{1,65},{2,18},{3,67},{4,20},{5,69},{6,22},{7,71},{8,24},{9,... | collective-permute-start | bytes 1179656 | tf_op jit(solution)/shard_map/ppermute | solution.py:438
  74.5 9.9 %collective-permute-start.9 = (s32[96,1024]{1,0:T(8,128)S(1)}, s32[96,1024]{1,0:T(8,128)S(1)}, u32[]{:S(2)}, u32[]{:S(2)}) collective-permute-start(s32[96,1024]{1,0:T(8,128)S(1)} %combine.6), channel_id=1, source_target_pairs={{0,8},{1,33},{2,10},{3,35},{4,12},{5,37},{6,14},{7,39},{8,16},{9,4... | collective-permute-start | bytes 1179656 | tf_op jit(solution)/shard_map/ppermute | solution.py:438
  79.7 7.8 %collective-permute-start.10 = (s32[96,1024]{1,0:T(8,128)S(1)}, s32[96,1024]{1,0:T(8,128)S(1)}, u32[]{:S(2)}, u32[]{:S(2)}) collective-permute-start(s32[96,1024]{1,0:T(8,128)S(1)} %combine.7), channel_id=1, source_target_pairs={{0,24},{1,97},{2,26},{3,99},{4,28},{5,101},{6,30},{7,103},{8,0},{9... | collective-permute-start | bytes 1179656 | tf_op jit(solution)/shard_map/ppermute | solution.py:438
